TPU v7x, 32 devices: a whole 2x2x4 slice. The times are simulated.
32 devices in a mesh: dp: 8 (over z, core), rows: 4 (over y, x).
Axes of the slice: x: 2, y: 2, z: 4, core: 2. Of those that a mesh axis runs over, the one named last changes fastest.
Arguments:
- tokens: bfloat16 [32, 32, 32, 768], P('dp', 'rows'), may hold values from -6 to 6
- conditioning: bfloat16 [32, 768], P('dp'), may hold values from -6 to 6
- item_map: int32 [32, 32, 32], P('dp'), may hold values from 0 to 3, as said below
- ada_weight: bfloat16 [768, 4608], P(('dp', 'rows')), may hold values from -0.21875 to 0.21875
- ada_bias: bfloat16 [4608], P(('dp', 'rows')), may hold values from -3 to 3
- attn_kernel: bfloat16 [9, 768], P(None, ('dp', 'rows')), may hold values from -2 to 2
- qkv_weight: bfloat16 [768, 2304], P(('dp', 'rows')), may hold values from -0.21875 to 0.21875
- out_weight: bfloat16 [768, 768], P(('dp', 'rows')), may hold values from -2 to 2
- up_weight: bfloat16 [768, 3072], P(('dp', 'rows')), may hold values from -0.21875 to 0.21875
- ffn_kernel: bfloat16 [9, 3072], P(None, ('dp', 'rows')), may hold values from -2 to 2
- down_weight: bfloat16 [3072, 768], P(('dp', 'rows')), may hold values from -0.109375 to 0.109375
- out_cotangent: bfloat16 [32, 32, 32, 768], P('dp', 'rows'), may hold values from -6 to 6
Outputs:
- layer_out: bfloat16 [32, 32, 32, 768], P('dp', 'rows')
- token_grad: float32 [32, 32, 32, 768], P('dp', 'rows')
- derivative_of_context: float32 [32, 768], P('dp')
- ada_weight_grad: float32 [768, 4608], P(('dp', 'rows'))
- ada_bias_grad: float32 [4608], P(('dp', 'rows'))
- attn_kernel_grad: float32 [9, 768], P(None, ('dp', 'rows'))
- derivative_triple_matrix: float32 [768, 2304], P(('dp', 'rows'))
- out_weight_grad: float32 [768, 768], P(('dp', 'rows'))
- up_weight_grad: float32 [768, 3072], P(('dp', 'rows'))
- ffn_kernel_grad: float32 [9, 3072], P(None, ('dp', 'rows'))
- down_weight_grad: float32 [3072, 768], P(('dp', 'rows'))
Inputs may be any that keep to these rules, and one draw needn't show every extreme that they name: `item_map`: in each canvas the labels 0 to 3 mark four latents, each a rectangle: 0 and 1 fill the first r rows, left and right of one column split; 2 and 3 fill the other rows, left and right of another split. r and both splits lie between 8 and 24, so every latent has 8 rows and columns or more.
All inputs are finite; a program needn't handle non-finite values.
Results may differ from a plain program's by a relative error of at most 0.019.
The roundings to bfloat16 on the way count: a program that leaves them out, or rounds other values in their place, can miss the bound.
Values may be sent and summed in bfloat16 or wider, within the bound.
A program may use at most 320 MiB of HBM per device.

v0:
```python
import jax
import jax.numpy as jnp
from jax import lax
from jax.sharding import PartitionSpec as P

PER_GROUP_WIDTH = 64


EPSILON = 1e-06


def padded(block, sides, width):
    for axis, dim in sides:
        count = lax.axis_size(axis)
        forward = [(i, i + 1) for i in range(count - 1)]
        backward = [(target, source) for source, target in forward]
        low = lax.ppermute(
            lax.slice_in_dim(block, block.shape[dim] - width, None, axis=dim), axis, forward
        )
        high = lax.ppermute(lax.slice_in_dim(block, 0, width, axis=dim), axis, backward)
        block = jnp.concatenate([low, block, high], axis=dim)
    return block


def normalize(attended_content_array):
    average = jnp.mean(attended_content_array, axis=-1, keepdims=True)
    centred = attended_content_array - average
    inverse = lax.rsqrt(jnp.mean(centred * centred, axis=-1, keepdims=True) + EPSILON)
    return (centred * inverse, inverse)


def normalize_back(incoming, normalized_rows, inverse):
    return inverse * (
        incoming
        - jnp.mean(incoming, axis=-1, keepdims=True)
        - normalized_rows * jnp.mean(incoming * normalized_rows, axis=-1, keepdims=True)
    )


def widen_cols(rimmed):
    return jnp.pad(rimmed, ((0, 0), (0, 0), (1, 1), (0, 0)))


def tap_mask(labels_pad, centre, row_off, col_off):
    rows_here = centre.shape[1]
    cols_here = centre.shape[2]
    return (labels_pad[:, row_off : row_off + rows_here, col_off : col_off + cols_here] == centre)[
        ..., None
    ]


def conv_forward(padded_rows, labels_pad, centre, kernel):
    rows_here = centre.shape[1]
    cols_here = centre.shape[2]
    summed = jnp.zeros(centre.shape + (kernel.shape[1],), jnp.float32)
    for row_off in range(3):
        for col_off in range(3):
            window = padded_rows[
                :, row_off : row_off + rows_here, col_off : col_off + cols_here
            ].astype(jnp.float32)
            tapped = kernel[3 * row_off + col_off].astype(jnp.float32) * window
            summed = summed + jnp.where(tap_mask(labels_pad, centre, row_off, col_off), tapped, 0.0)
    return summed


def conv_mirror(padded_rows, labels_pad, centre, kernel):
    rows_here = centre.shape[1]
    cols_here = centre.shape[2]
    summed = jnp.zeros(centre.shape + (kernel.shape[1],), jnp.float32)
    for row_off in range(3):
        for col_off in range(3):
            row_from = 2 - row_off
            col_from = 2 - col_off
            window = padded_rows[
                :, row_from : row_from + rows_here, col_from : col_from + cols_here
            ].astype(jnp.float32)
            tapped = kernel[3 * row_off + col_off].astype(jnp.float32) * window
            summed = summed + jnp.where(
                tap_mask(labels_pad, centre, row_from, col_from), tapped, 0.0
            )
    return summed


def kernel_grad(incoming, padded_rows, labels_pad, centre):
    rows_here = centre.shape[1]
    cols_here = centre.shape[2]
    incoming_values = incoming.astype(jnp.float32)
    tap_sums = []
    for row_off in range(3):
        for col_off in range(3):
            window = padded_rows[
                :, row_off : row_off + rows_here, col_off : col_off + cols_here
            ].astype(jnp.float32)
            product = jnp.where(
                tap_mask(labels_pad, centre, row_off, col_off), incoming_values * window, 0.0
            )
            tap_sums.append(jnp.sum(product, axis=(0, 1, 2)))
    return jnp.stack(tap_sums, axis=0)


def contract_rows(left, right):
    return lax.dot_general(
        left, right, (((0,), (0,)), ((), ())), preferred_element_type=jnp.float32
    )


def contract_cols(left, right):
    return lax.dot_general(
        left, right, (((1,), (1,)), ((), ())), preferred_element_type=jnp.float32
    )


def local(
    tokens,
    conditioning,
    item_map,
    ada_weight,
    ada_bias,
    attn_kernel,
    qkv_weight,
    out_weight,
    up_weight,
    ffn_kernel,
    down_weight,
    out_cotangent,
):
    canvases, rows_here, cols_here, features = tokens.shape
    cell_count = canvases * rows_here * cols_here
    position = lax.axis_index("rows")
    gathered = (
        lax.all_gather(ada_weight, ("dp", "rows"), axis=0, tiled=True),
        lax.all_gather(ada_bias, ("dp", "rows"), axis=0, tiled=True),
        lax.all_gather(attn_kernel, ("dp", "rows"), axis=1, tiled=True),
        lax.all_gather(qkv_weight, ("dp", "rows"), axis=0, tiled=True),
        lax.all_gather(out_weight, ("dp", "rows"), axis=0, tiled=True),
        lax.all_gather(up_weight, ("dp", "rows"), axis=0, tiled=True),
        lax.all_gather(ffn_kernel, ("dp", "rows"), axis=1, tiled=True),
        lax.all_gather(down_weight, ("dp", "rows"), axis=0, tiled=True),
    )
    ada_full, bias_full, kernel_attn, triple_full, out_full, up_full, kernel_ffn, down_full = (
        gathered
    )
    hidden_units = up_full.shape[1]
    head_count = features // PER_GROUP_WIDTH
    logit_divisor = PER_GROUP_WIDTH ** (-0.5)
    labels_pad = jnp.pad(item_map, ((0, 0), (1, 1), (1, 1)), constant_values=-1)
    labels_here = lax.dynamic_slice_in_dim(labels_pad, position * rows_here, rows_here + 2, 1)
    centre = labels_here[:, 1:-1, 1:-1]
    cond_values = conditioning.astype(jnp.float32)
    silu_low = jax.nn.silu(cond_values).astype(jnp.bfloat16)
    modulation = jnp.dot(silu_low, ada_full, preferred_element_type=jnp.float32) + bias_full.astype(
        jnp.float32
    )
    layer_stack = modulation.reshape(canvases, 6, 1, 1, features)
    shift_one, scale_one, gate_one, shift_two, scale_two, gate_two = (
        layer_stack[:, index] for index in range(6)
    )
    token_values = tokens.astype(jnp.float32)
    normed_one, inverse_one = normalize(token_values)
    modulated_one = (normed_one * (1.0 + scale_one) + shift_one).astype(jnp.bfloat16)
    modulated_padded = widen_cols(padded(modulated_one, (("rows", 1),), 1))
    local_mix = conv_forward(modulated_padded, labels_here, centre, kernel_attn).astype(
        jnp.bfloat16
    )
    mix_rows = local_mix.reshape(cell_count, features)
    projected = jnp.dot(mix_rows, triple_full, preferred_element_type=jnp.float32).astype(
        jnp.bfloat16
    )
    projected = projected.reshape(canvases, rows_here * cols_here, 3 * features)
    queries = projected[..., :features]
    key_rows = projected[..., features : 2 * features]
    value_rows = projected[..., 2 * features :]
    keys_all, values_all = (
        lax.all_gather(key_rows, "rows", axis=1, tiled=True),
        lax.all_gather(value_rows, "rows", axis=1, tiled=True),
    )
    query_heads = queries.reshape(canvases, -1, head_count, PER_GROUP_WIDTH)
    key_heads = keys_all.reshape(canvases, -1, head_count, PER_GROUP_WIDTH)
    value_heads = values_all.reshape(canvases, -1, head_count, PER_GROUP_WIDTH)
    scores = (
        jnp.einsum("bqhd,bkhd->bhqk", query_heads, key_heads, preferred_element_type=jnp.float32)
        * logit_divisor
    )
    label_rows = centre.reshape(canvases, -1)
    label_keys = item_map.reshape(canvases, -1)
    linked = label_rows[:, None, :, None] == label_keys[:, None, None, :]
    masked = jnp.where(linked, scores, -1e30)
    row_peak = jnp.max(masked, axis=-1, keepdims=True)
    raised = jnp.exp(masked - row_peak)
    row_total = jnp.sum(raised, axis=-1, keepdims=True)
    attention = raised / row_total
    attention_low = attention.astype(jnp.bfloat16)
    attended = jnp.einsum(
        "bhqk,bkhd->bqhd", attention_low, value_heads, preferred_element_type=jnp.float32
    ).astype(jnp.bfloat16)
    attended = attended.reshape(cell_count, features)
    attn_branch = jnp.dot(attended, out_full, preferred_element_type=jnp.float32).reshape(
        tokens.shape
    )
    middle = token_values + gate_one * attn_branch
    normed_two, inverse_two = normalize(middle)
    modulated_two = (normed_two * (1.0 + scale_two) + shift_two).astype(jnp.bfloat16)
    modulated_rows = modulated_two.reshape(cell_count, features)
    hidden_up_projection = jnp.dot(
        modulated_rows, up_full, preferred_element_type=jnp.float32
    ).astype(jnp.bfloat16)
    hidden_up_projection = hidden_up_projection.reshape(
        canvases, rows_here, cols_here, hidden_units
    )
    up_padded = widen_cols(padded(hidden_up_projection, (("rows", 1),), 1))
    pre_gelu = conv_forward(up_padded, labels_here, centre, kernel_ffn)
    activated, gelu_back = jax.vjp(jax.nn.gelu, pre_gelu)
    gelu_low = activated.astype(jnp.bfloat16).reshape(cell_count, hidden_units)
    ffn_branch = jnp.dot(gelu_low, down_full, preferred_element_type=jnp.float32).reshape(
        tokens.shape
    )
    layer_out = (middle + gate_two * ffn_branch).astype(jnp.bfloat16)
    weights_back = (
        lax.all_gather(ada_weight, ("dp", "rows"), axis=0, tiled=True),
        lax.all_gather(ada_bias, ("dp", "rows"), axis=0, tiled=True),
        lax.all_gather(attn_kernel, ("dp", "rows"), axis=1, tiled=True),
        lax.all_gather(qkv_weight, ("dp", "rows"), axis=0, tiled=True),
        lax.all_gather(out_weight, ("dp", "rows"), axis=0, tiled=True),
        lax.all_gather(up_weight, ("dp", "rows"), axis=0, tiled=True),
        lax.all_gather(ffn_kernel, ("dp", "rows"), axis=1, tiled=True),
        lax.all_gather(down_weight, ("dp", "rows"), axis=0, tiled=True),
    )
    (
        ada_back,
        bias_back,
        kernel_attn_back,
        triple_back,
        out_back,
        up_back,
        kernel_ffn_back,
        down_projection_back,
    ) = weights_back
    incoming = out_cotangent.astype(jnp.float32)
    grad_gate_two = jnp.sum(incoming * ffn_branch, axis=(1, 2))
    grad_ffn = (gate_two * incoming).astype(jnp.bfloat16).reshape(cell_count, features)
    grad_down = contract_rows(gelu_low, grad_ffn)
    grad_gelu = contract_cols(grad_ffn, down_projection_back).reshape(
        canvases, rows_here, cols_here, hidden_units
    )
    grad_pre = gelu_back(grad_gelu)[0].astype(jnp.bfloat16)
    grad_pre_padded = widen_cols(padded(grad_pre, (("rows", 1),), 1))
    grad_kernel_ffn = kernel_grad(grad_pre, up_padded, labels_here, centre)
    grad_up = (
        conv_mirror(grad_pre_padded, labels_here, centre, kernel_ffn_back)
        .astype(jnp.bfloat16)
        .reshape(cell_count, hidden_units)
    )
    grad_up_weight = contract_rows(modulated_rows, grad_up)
    grad_mod_two = contract_cols(grad_up, up_back).reshape(tokens.shape)
    grad_scale_two = jnp.sum(grad_mod_two * normed_two, axis=(1, 2))
    grad_shift_two = jnp.sum(grad_mod_two, axis=(1, 2))
    grad_middle = incoming + normalize_back(
        grad_mod_two * (1.0 + scale_two), normed_two, inverse_two
    )
    grad_gate_one = jnp.sum(grad_middle * attn_branch, axis=(1, 2))
    grad_attn = (gate_one * grad_middle).astype(jnp.bfloat16).reshape(cell_count, features)
    grad_out_weight = contract_rows(attended, grad_attn)
    grad_attended = (
        contract_cols(grad_attn, out_back)
        .astype(jnp.bfloat16)
        .reshape(canvases, -1, head_count, PER_GROUP_WIDTH)
    )
    grad_weights = jnp.einsum(
        "bqhd,bkhd->bhqk", grad_attended, value_heads, preferred_element_type=jnp.float32
    )
    row_delta = jnp.sum(attention * grad_weights, axis=-1, keepdims=True)
    grad_scores = (attention * (grad_weights - row_delta)).astype(jnp.bfloat16)
    grad_query = (
        jnp.einsum("bhqk,bkhd->bqhd", grad_scores, key_heads, preferred_element_type=jnp.float32)
        * logit_divisor
    )
    grad_key_all = (
        jnp.einsum("bhqk,bqhd->bkhd", grad_scores, query_heads, preferred_element_type=jnp.float32)
        * logit_divisor
    )
    value_gradient_full = jnp.einsum(
        "bhqk,bqhd->bkhd", attention_low, grad_attended, preferred_element_type=jnp.float32
    )
    grad_key, grad_value = (
        lax.psum_scatter(
            grad_key_all.reshape(canvases, -1, features).astype(jnp.bfloat16),
            "rows",
            scatter_dimension=1,
            tiled=True,
        ).astype(jnp.float32),
        lax.psum_scatter(
            value_gradient_full.reshape(canvases, -1, features).astype(jnp.bfloat16),
            "rows",
            scatter_dimension=1,
            tiled=True,
        ).astype(jnp.float32),
    )
    grad_projected = jnp.concatenate(
        [
            grad_query.reshape(cell_count, features),
            grad_key.reshape(cell_count, features),
            grad_value.reshape(cell_count, features),
        ],
        axis=-1,
    ).astype(jnp.bfloat16)
    grad_qkv_weight = contract_rows(mix_rows, grad_projected)
    grad_mix = contract_cols(grad_projected, triple_back).astype(jnp.bfloat16).reshape(tokens.shape)
    grad_mix_padded = widen_cols(padded(grad_mix, (("rows", 1),), 1))
    grad_kernel_attn = kernel_grad(grad_mix, modulated_padded, labels_here, centre)
    grad_mod_one = conv_mirror(grad_mix_padded, labels_here, centre, kernel_attn_back)
    grad_scale_one = jnp.sum(grad_mod_one * normed_one, axis=(1, 2))
    grad_shift_one = jnp.sum(grad_mod_one, axis=(1, 2))
    token_grad = grad_middle + normalize_back(
        grad_mod_one * (1.0 + scale_one), normed_one, inverse_one
    )
    grad_parts = jnp.concatenate(
        [
            grad_shift_one,
            grad_scale_one,
            grad_gate_one,
            grad_shift_two,
            grad_scale_two,
            grad_gate_two,
        ],
        axis=-1,
    )
    grad_modulation = lax.psum(grad_parts.astype(jnp.bfloat16), "rows")
    leader = (position == 0).astype(jnp.float32)
    grad_ada_weight = contract_rows(silu_low, grad_modulation) * leader
    grad_ada_bias = jnp.sum(grad_modulation.astype(jnp.float32), axis=0) * leader
    silu_values, silu_back = jax.vjp(jax.nn.silu, cond_values)
    derivative_of_context = silu_back(contract_cols(grad_modulation, ada_back))[0]
    summed_grads = (
        lax.psum_scatter(grad_ada_weight, ("dp", "rows"), scatter_dimension=0, tiled=True),
        lax.psum_scatter(grad_ada_bias, ("dp", "rows"), scatter_dimension=0, tiled=True),
        lax.psum_scatter(grad_kernel_attn, ("dp", "rows"), scatter_dimension=1, tiled=True),
        lax.psum_scatter(grad_qkv_weight, ("dp", "rows"), scatter_dimension=0, tiled=True),
        lax.psum_scatter(grad_out_weight, ("dp", "rows"), scatter_dimension=0, tiled=True),
        lax.psum_scatter(grad_up_weight, ("dp", "rows"), scatter_dimension=0, tiled=True),
        lax.psum_scatter(grad_kernel_ffn, ("dp", "rows"), scatter_dimension=1, tiled=True),
        lax.psum_scatter(grad_down, ("dp", "rows"), scatter_dimension=0, tiled=True),
    )
    return (layer_out, token_grad, derivative_of_context) + tuple(summed_grads)


def solution(mesh):
    return jax.shard_map(
        local,
        mesh=mesh,
        in_specs=(
            P("dp", "rows", None, None),
            P("dp", None),
            P("dp", None, None),
            P(("dp", "rows"), None),
            P(("dp", "rows")),
            P(None, ("dp", "rows")),
            P(("dp", "rows"), None),
            P(("dp", "rows"), None),
            P(("dp", "rows"), None),
            P(None, ("dp", "rows")),
            P(("dp", "rows"), None),
            P("dp", "rows", None, None),
        ),
        out_specs=(
            P("dp", "rows", None, None),
            P("dp", "rows", None, None),
            P("dp", None),
            P(("dp", "rows"), None),
            P(("dp", "rows")),
            P(None, ("dp", "rows")),
            P(("dp", "rows"), None),
            P(("dp", "rows"), None),
            P(("dp", "rows"), None),
            P(None, ("dp", "rows")),
            P(("dp", "rows"), None),
        ),
        check_vma=False,
    )
```

profile of v0, /device:TPU:0, one launch (start us, length us, event | category | flops | bytes accessed | tf_op | source)
XLA Modules:
  0.0 1699.0 jit_solution(1797538843501480399)
XLA Ops:
  9.6 42.7 %all-reduce.5 = bf16[4608]{0:T(1024)(128)(2,1)S(1)} all-reduce(bf16[4608]{0:T(1024)(128)(2,1)S(1)} %dynamic-update-slice), channel_id=1, replica_groups=mesh['dp'=8,'rows'=4] {'dp','rows'}, use_global_device_ids=true, to_apply=%add.5 | all-reduce | flops 4608 | bytes 18432
  52.3 68.0 %all-gather = bf16[32,24,9]{1,2,0:T(8,128)(2,1)S(1)} all-gather(bf16[1,24,9]{1,2,0:T(8,128)(2,1)} %bitcast.227), channel_id=1, replica_groups=mesh['dp'=8,'rows'=4] {'dp','rows'}, dimensions={0}, use_global_device_ids=true | all-gather | bytes 14256 | tf_op jit(solution)/shard_map/all_gather | solution.py:133
  167.6 60.1 %all-gather.16.cloned.1.call-done = bf16[4,1024,768]{2,1,0:T(8,128)(2,1)} async-done(((bf16[4,256,768]{2,1,0:T(8,128)(2,1)}), bf16[4,1024,768]{2,1,0:T(8,128)(2,1)}) %all-gather.16.cloned.1.call-update) | async-done | bytes 6291472 | tf_op jit(solution)/shard_map/all_gather | solution.py:174
  236.3 24.8 %fusion.181 = (f32[4,12,256]{2,1,0:T(8,128)S(1)}, f32[4,12,256,1024]{3,2,1,0:T(8,128)}) fusion(pred[4,256,1024]{2,1,0:T(8,128)(4,1)} %broadcast_compare_fusion, bf16[4,256,12,64]{1,3,2,0:T(8,128)(2,1)S(1)} %bitcast.168, bf16[4,1024,12,64]{1,3,2,0:T(8,128)(2,1)} %bitcast.165), kind=kOutput, calls=%fused_computation.316 | convolution fusion | flops 1660945408 | bytes 59293696 | tf_op jit(solution)/shard_map/sub | solution.py:189
  261.1 38.3 %all-gather.14.cloned.1.call-done = bf16[4,1024,768]{2,1,0:T(8,128)(2,1)} async-done(((bf16[4,256,768]{2,1,0:T(8,128)(2,1)}), bf16[4,1024,768]{2,1,0:T(8,128)(2,1)}) %all-gather.14.cloned.1.call-update) | async-done | bytes 6291472 | tf_op jit(solution)/shard_map/all_gather | solution.py:175
  308.1 20.2 %fusion.133 = bf16[4,256,12,64]{1,3,2,0:T(8,128)(2,1)S(1)} fusion(bf16[4,1024,12,64]{1,3,2,0:T(8,128)(2,1)} %bitcast.170, f32[4,12,256,1024]{3,2,1,0:T(8,128)} %get-tuple-element.93, f32[4,12,256]{2,1,0:T(8,128)S(1)} %get-tuple-element.92), kind=kOutput, calls=%fused_computation.219 | convolution fusion | flops 1636564992 | bytes 58245120 | tf_op jit(solution)/shard_map/bhqk,bkhd->bqhd/dot_general | solution.py:193
  339.1 17.1 %all-gather.18.cloned.1.call-done = bf16[768,768]{1,0:T(8,128)(2,1)} async-done(((bf16[24,768]{1,0:T(8,128)(2,1)}), bf16[768,768]{1,0:T(8,128)(2,1)}) %all-gather.18.cloned.1.call-update) | async-done | bytes 1179664 | tf_op jit(solution)/shard_map/all_gather | solution.py:135
  363.9 57.5 %all-gather.20.cloned.1.call-done = bf16[768,3072]{1,0:T(8,128)(2,1)} async-done(((bf16[24,3072]{1,0:T(8,128)(2,1)}), bf16[768,3072]{1,0:T(8,128)(2,1)}) %all-gather.20.cloned.1.call-update) | async-done | bytes 4718608 | tf_op jit(solution)/shard_map/all_gather | solution.py:136
  436.6 101.5 %all-gather.1 = bf16[32,96,9]{1,2,0:T(8,128)(2,1)S(1)} all-gather(bf16[1,96,9]{1,2,0:T(8,128)(2,1)S(1)} %bitcast.228), channel_id=1, replica_groups=mesh['dp'=8,'rows'=4] {'dp','rows'}, dimensions={0}, use_global_device_ids=true | all-gather | bytes 57024 | tf_op jit(solution)/shard_map/all_gather | solution.py:137
  550.2 24.5 %fusion.14 = f32[4,8,32,3072]{3,2,1,0:T(8,128)} fusion(bf16[4,8,32,3072]{3,2,1,0:T(8,128)(2,1)S(1)} %bitcast.161, bf16[4,1,32,3072]{3,2,1,0:T(8,128)(2,1)S(1)} %collective-permute-done.3, bf16[4,1,32,3072]{3,2,1,0:T(8,128)(2,1)S(1)} %collective-permute-done.2, f32[3072]{0:T(1024)S(1)} %bitcast.194, f32[3072]{0:T(1024)S(1)} %bitcast.196, ...), kind=kLoop, calls=%fused_computation.42 | loop fusion | flops 113246208 | bytes 58314752 | tf_op jit(solution)/shard_map/add | solution.py:62
  574.7 39.3 %fusion.51 = (f32[3072]{0:T(1024)}, f32[3072]{0:T(1024)}, f32[3072]{0:T(1024)}, f32[3072]{0:T(1024)}, f32[3072]{0:T(1024)}, /*index=5*/f32[3072]{0:T(1024)}, f32[3072]{0:T(1024)}, bf16[4,8,32,3072]{3,2,1,0:T(8,128)(2,1)S(1)}) fusion(pred[4,8,32]{2,1,0:T(8,128)(4,1)S(1)} %get-tuple-element.86, bf16[4,10,34,3072]{3,2,1,0:T(8,128)(2,1)} %copy-done, ...), kind=kOutput, calls=%fused_computation.79 | convolution fusion | flops 4985170944 | bytes 69310464 | tf_op jit(solution)/shard_map/dot_general | solution.py:108
  619.4 10.0 collective-permute-done.4
  629.4 17.6 %collective-permute-done.5 = bf16[4,1,32,3072]{3,2,1,0:T(8,128)(2,1)S(1)} collective-permute-done((bf16[4,1,32,3072]{3,2,1,0:T(8,128)(2,1)S(1)}, bf16[4,1,32,3072]{3,2,1,0:T(8,128)(2,1)S(1)}, u32[]{:S(2)}, u32[]{:S(2)}) %collective-permute-start.5) | collective-permute-done | bytes 786464 | tf_op jit(solution)/shard_map/ppermute | solution.py:20
  652.3 23.7 %fusion.34 = bf16[4,8,32,3072]{3,2,1,0:T(8,128)(2,1)S(1)} fusion(bf16[4,8,32,3072]{3,2,1,0:T(8,128)(2,1)S(1)} %get-tuple-element.99, bf16[4,10,34,3072]{3,2,1,0:T(8,128)(2,1)S(1)} %select_maximum_fusion, bf16[4,1,32,3072]{3,2,1,0:T(8,128)(2,1)S(1)} %collective-permute-done.4, bf16[4,1,32,3072]{3,2,1,0:T(8,128)(2,1)S(1)} %collective-permute-done.5, ...), kind=kLoop, calls=%fused_computation.62 | loop fusion | flops 116391936 | bytes 52023296 | tf_op jit(solution)/shard_map/convert_element_type | solution.py:250
  676.0 12.6 multiply_reduce_fusion.1
  688.6 14.9 fusion.103
  710.1 20.2 %fusion.74 = bf16[4,12,64,1024]{3,2,1,0:T(8,128)(2,1)} fusion(bf16[4,256,12,64]{1,0,3,2:T(4,128)(2,1)S(1)} %reshape.306, f32[4,12,256,1024]{3,2,1,0:T(8,128)} %get-tuple-element.93, f32[4,12,256]{2,1,0:T(8,128)S(1)} %get-tuple-element.92), kind=kOutput, calls=%fused_computation.143 | convolution fusion | flops 1638924288 | bytes 58245120 | tf_op jit(solution)/shard_map/bhqk,bqhd->bkhd/dot_general | solution.py:281
  739.0 35.8 %multiply_reduce_fusion = (f32[4,12,256]{2,1,0:T(8,128)S(1)}, f32[4,12,256,1024]{3,2,1,0:T(8,128)}) fusion(f32[4,12,256,1024]{3,2,1,0:T(8,128)} %get-tuple-element.93, f32[4,12,256]{2,1,0:T(8,128)S(1)} %get-tuple-element.92, bf16[4,1024,12,64]{1,3,2,0:T(8,128)(2,1)} %bitcast.171, bf16[4,256,12,64]{1,0,3,2:T(4,128)(2,1)S(1)} %reshape.306), kind=kOutput, calls=%fused_computation.2 | convolution fusion | flops 1648349184 | bytes 108625920 | tf_op jit(solution)/shard_map/bqhd,bkhd->bhqk/dot_general | solution.py:268
  774.7 41.5 %multiply_convert_fusion = bf16[4,12,256,1024]{3,2,1,0:T(8,128)(2,1)} fusion(f32[4,12,256,1024]{3,2,1,0:T(8,128)} %get-tuple-element.97, f32[4,12,256]{2,1,0:T(8,128)S(1)} %get-tuple-element.96, f32[4,12,256,1024]{3,2,1,0:T(8,128)} %get-tuple-element.93, f32[4,12,256]{2,1,0:T(8,128)S(1)} %get-tuple-element.92), kind=kLoop, calls=%fused_computation.1 | loop fusion | flops 50331648 | bytes 125927424 | tf_op jit(solution)/shard_map/convert_element_type | solution.py:272
  816.2 15.2 multiply_convert_fusion.1
  857.4 13.7 convolution_bitcast_fusion
  872.4 10.4 convolution_bitcast_fusion.1
  882.9 15.1 fusion.136
  921.5 10.1 fusion.125
  959.2 15.3 psum.7
  982.4 29.5 %reduce-scatter.26.cloned.1.call-done = f32[96,9]{1,0:T(8,128)} async-done(((f32[3072,9]{1,0:T(8,128)}), f32[96,9]{1,0:T(8,128)}) %reduce-scatter.26.cloned.1.call-update) | async-done | bytes 3472
  1017.0 41.1 %all-reduce.8 = (f32[4608]{0:T(1024)S(1)}, f32[9,768]{1,0:T(8,128)S(1)}) all-reduce(f32[4608]{0:T(1024)S(1)} %broadcast_multiply_fusion, f32[9,768]{1,0:T(8,128)S(1)} %stack.69), channel_id=5, replica_groups=mesh['dp'=8,'rows'=4] {'dp','rows'}, use_global_device_ids=true, to_apply=%region_22.23.clone | all-reduce | flops 11520 | bytes 92160
  1069.0 47.5 %reduce-scatter.20.cloned.1.call-done = f32[24,768]{1,0:T(8,128)} async-done(((f32[768,768]{1,0:T(8,128)}), f32[24,768]{1,0:T(8,128)}) %reduce-scatter.20.cloned.1.call-update) | async-done | bytes 73744 | tf_op jit(solution)/shard_map/reduce_scatter | solution.py:338
  1116.4 141.5 %reduce-scatter.24.cloned.1.call-done = f32[96,768]{1,0:T(8,128)} async-done(((f32[3072,768]{1,0:T(8,128)}), f32[96,768]{1,0:T(8,128)}) %reduce-scatter.24.cloned.1.call-update) | async-done | bytes 294928 | tf_op jit(solution)/shard_map/reduce_scatter | solution.py:341
  1257.9 141.7 %reduce-scatter.22.cloned.1.call-done = f32[24,3072]{1,0:T(8,128)} async-done(((f32[768,3072]{1,0:T(8,128)}), f32[24,3072]{1,0:T(8,128)}) %reduce-scatter.22.cloned.1.call-update) | async-done | bytes 294928 | tf_op jit(solution)/shard_map/reduce_scatter | solution.py:339
  1399.6 124.7 %reduce-scatter.18.cloned.1.call-done = f32[24,2304]{1,0:T(8,128)} async-done(((f32[768,2304]{1,0:T(8,128)}), f32[24,2304]{1,0:T(8,128)}) %reduce-scatter.18.cloned.1.call-update) | async-done | bytes 221200 | tf_op jit(solution)/shard_map/reduce_scatter | solution.py:337
  1524.3 168.0 %reduce-scatter.16.cloned.1.call-done = f32[24,4608]{1,0:T(8,128)} async-done(((f32[768,4608]{1,0:T(8,128)}), f32[24,4608]{1,0:T(8,128)}) %reduce-scatter.16.cloned.1.call-update) | async-done | bytes 442384 | tf_op jit(solution)/shard_map/reduce_scatter | solution.py:334
  (374 shorter events, 239.1 us)
Async XLA Ops:
  7.2 116.8 %all-gather.10.cloned.1.call-start = ((), (), s32[]{:S(2)}) async-start(), calls=%async_computation.8 | async-start | bytes 7299072 | tf_op jit(solution)/shard_map/all_gather | solution.py:131
  7.9 144.1 %all-gather.12.cloned.1.call-start = ((), (), s32[]{:S(2)}) async-start(), calls=%async_computation.9 | async-start | bytes 3649536 | tf_op jit(solution)/shard_map/all_gather | solution.py:134
  8.7 219.0 %all-gather.16.cloned.1.call-start = ((), (), s32[]{:S(2)}) async-start(), calls=%async_computation.11 | async-start | bytes 7864320 | tf_op jit(solution)/shard_map/all_gather | solution.py:174
  121.5 530.7 %copy-start.69 = (pred[4,8,32]{2,1,0:T(8,128)(4,1)}, pred[4,8,32]{2,1,0:T(8,128)(4,1)S(1)}, u32[]{:S(2)}) copy-start(pred[4,8,32]{2,1,0:T(8,128)(4,1)S(1)} %get-tuple-element.53) | copy-start | bytes 3076
  129.5 9.6 collective-permute-start
  131.7 11.8 collective-permute-start.1
  133.2 519.0 %copy-start.45 = (pred[4,8,32]{2,1,0:T(8,128)(4,1)}, pred[4,8,32]{2,1,0:T(8,128)(4,1)S(1)}, u32[]{:S(2)}) copy-start(pred[4,8,32]{2,1,0:T(8,128)(4,1)S(1)} %get-tuple-element.85) | copy-start | bytes 3076
  133.2 519.0 %copy-start.48 = (pred[4,8,32]{2,1,0:T(8,128)(4,1)}, pred[4,8,32]{2,1,0:T(8,128)(4,1)S(1)}, u32[]{:S(2)}) copy-start(pred[4,8,32]{2,1,0:T(8,128)(4,1)S(1)} %get-tuple-element.87) | copy-start | bytes 3076
  133.2 519.0 %copy-start.54 = (pred[4,8,32]{2,1,0:T(8,128)(4,1)}, pred[4,8,32]{2,1,0:T(8,128)(4,1)S(1)}, u32[]{:S(2)}) copy-start(pred[4,8,32]{2,1,0:T(8,128)(4,1)S(1)} %get-tuple-element.86) | copy-start | bytes 3076
  133.2 519.0 %copy-start.57 = (pred[4,8,32]{2,1,0:T(8,128)(4,1)}, pred[4,8,32]{2,1,0:T(8,128)(4,1)S(1)}, u32[]{:S(2)}) copy-start(pred[4,8,32]{2,1,0:T(8,128)(4,1)S(1)} %get-tuple-element.88) | copy-start | bytes 3076
  133.2 519.0 %copy-start.60 = (pred[4,8,32]{2,1,0:T(8,128)(4,1)}, pred[4,8,32]{2,1,0:T(8,128)(4,1)S(1)}, u32[]{:S(2)}) copy-start(pred[4,8,32]{2,1,0:T(8,128)(4,1)S(1)} %get-tuple-element.89) | copy-start | bytes 3076
  133.2 519.0 %copy-start.63 = (pred[4,8,32]{2,1,0:T(8,128)(4,1)}, pred[4,8,32]{2,1,0:T(8,128)(4,1)S(1)}, u32[]{:S(2)}) copy-start(pred[4,8,32]{2,1,0:T(8,128)(4,1)S(1)} %get-tuple-element.90) | copy-start | bytes 3076
  133.3 519.0 %copy-start.66 = (pred[4,8,32]{2,1,0:T(8,128)(4,1)}, pred[4,8,32]{2,1,0:T(8,128)(4,1)S(1)}, u32[]{:S(2)}) copy-start(pred[4,8,32]{2,1,0:T(8,128)(4,1)S(1)} %get-tuple-element.91) | copy-start | bytes 3076
  161.0 138.5 %all-gather.14.cloned.1.call-start = ((), (), s32[]{:S(2)}) async-start(), calls=%async_computation.10 | async-start | bytes 7864320 | tf_op jit(solution)/shard_map/all_gather | solution.py:175
  161.5 194.6 %all-gather.18.cloned.1.call-start = ((), (), s32[]{:S(2)}) async-start(), calls=%async_computation.12 | async-start | bytes 1216512 | tf_op jit(solution)/shard_map/all_gather | solution.py:135
  162.1 259.2 %all-gather.20.cloned.1.call-start = ((), (), s32[]{:S(2)}) async-start(), calls=%async_computation.13 | async-start | bytes 4866048 | tf_op jit(solution)/shard_map/all_gather | solution.py:136
  162.7 412.0 %all-gather.22.cloned.1.call-start = ((), (), s32[]{:S(2)}) async-start(), calls=%async_computation.14 | async-start | bytes 4866048 | tf_op jit(solution)/shard_map/all_gather | solution.py:138
  163.5 736.2 %reduce-scatter.14.cloned.1.call-start = ((), (), s32[]{:S(2)}) async-start(), calls=%async_computation.16 | async-start | bytes 7864320 | tf_op jit(solution)/shard_map/reduce_scatter | solution.py:291
  431.9 106.5 %collective-permute-start.2 = (bf16[4,1,32,3072]{3,2,1,0:T(8,128)(2,1)S(1)}, bf16[4,1,32,3072]{3,2,1,0:T(8,128)(2,1)S(1)}, u32[]{:S(2)}, u32[]{:S(2)}) collective-permute-start(bf16[4,1,32,3072]{3,2,1,0:T(8,128)(2,1)S(1)} %get-tuple-element.57), channel_id=1, source_target_pairs={{0,1},{1,2},{2,3},{4,5},{5,6},{6,7},{8,9},{9,10},{10,11},{12,13},{... | collective-permute-start | bytes 2359304 | tf_op jit(solution)/shard_map/ppermute | solution.py:17
  435.3 103.1 %collective-permute-start.3 = (bf16[4,1,32,3072]{3,2,1,0:T(8,128)(2,1)S(1)}, bf16[4,1,32,3072]{3,2,1,0:T(8,128)(2,1)S(1)}, u32[]{:S(2)}, u32[]{:S(2)}) collective-permute-start(bf16[4,1,32,3072]{3,2,1,0:T(8,128)(2,1)S(1)} %get-tuple-element.58), channel_id=1, source_target_pairs={{1,0},{2,1},{3,2},{5,4},{6,5},{7,6},{9,8},{10,9},{11,10},{13,12},{... | collective-permute-start | bytes 2359304 | tf_op jit(solution)/shard_map/ppermute | solution.py:20
  538.4 150.2 %copy-start.104 = (f32[4,1,1,1,768]{4,0,1,3,2:T(4,128)}, f32[4,1,1,1,768]{4,0,1,3,2:T(4,128)S(1)}, u32[]{:S(2)}) copy-start(f32[4,1,1,1,768]{4,0,1,3,2:T(4,128)S(1)} %copy.104) | copy-start | bytes 36868
  614.2 15.2 collective-permute-start.4
  618.1 28.9 %collective-permute-start.5 = (bf16[4,1,32,3072]{3,2,1,0:T(8,128)(2,1)S(1)}, bf16[4,1,32,3072]{3,2,1,0:T(8,128)(2,1)S(1)}, u32[]{:S(2)}, u32[]{:S(2)}) collective-permute-start(bf16[4,1,32,3072]{3,2,1,0:T(8,128)(2,1)S(1)} %get-tuple-element.56), channel_id=1, source_target_pairs={{1,0},{2,1},{3,2},{5,4},{6,5},{7,6},{9,8},{10,9},{11,10},{13,12},{... | collective-permute-start | bytes 2359304 | tf_op jit(solution)/shard_map/ppermute | solution.py:20
  738.9 169.6 %reduce-scatter.12.cloned.1.call-start = ((), (), s32[]{:S(2)}) async-start(), calls=%async_computation.15 | async-start | bytes 7864320 | tf_op jit(solution)/shard_map/reduce_scatter | solution.py:285
  840.1 171.7 %reduce-scatter.26.cloned.1.call-start = ((), (), s32[]{:S(2)}) async-start(), calls=%async_computation.22 | async-start | bytes 1622016
  854.4 262.1 %reduce-scatter.20.cloned.1.call-start = ((), (), s32[]{:S(2)}) async-start(), calls=%async_computation.19 | async-start | bytes 2433024 | tf_op jit(solution)/shard_map/reduce_scatter | solution.py:338
  857.3 400.6 %reduce-scatter.24.cloned.1.call-start = ((), (), s32[]{:S(2)}) async-start(), calls=%async_computation.21 | async-start | bytes 9732096 | tf_op jit(solution)/shard_map/reduce_scatter | solution.py:341
  871.1 528.6 %reduce-scatter.22.cloned.1.call-start = ((), (), s32[]{:S(2)}) async-start(), calls=%async_computation.20 | async-start | bytes 9732096 | tf_op jit(solution)/shard_map/reduce_scatter | solution.py:339
  882.8 641.5 %reduce-scatter.18.cloned.1.call-start = ((), (), s32[]{:S(2)}) async-start(), calls=%async_computation.18 | async-start | bytes 7299072 | tf_op jit(solution)/shard_map/reduce_scatter | solution.py:337
  919.8 772.4 %reduce-scatter.16.cloned.1.call-start = ((), (), s32[]{:S(2)}) async-start(), calls=%async_computation.17 | async-start | bytes 14598144 | tf_op jit(solution)/shard_map/reduce_scatter | solution.py:334
  933.6 7.8 collective-permute-start.6
  937.1 10.3 collective-permute-start.7
  (105 other events, 1433.4 us)
Sparse Core Ops, SparseCore 0:
  10.9 75.8 all-gather.9
  89.7 59.5 all-gather.11
  161.1 66.5 all-gather.15
  229.4 70.0 all-gather.13
  302.2 53.9 all-gather.17
  358.9 62.3 all-gather.19
  424.3 69.1 all-gather.21
  739.0 66.8 reduce-scatter.13
  840.2 68.2 reduce-scatter.11
  913.6 98.1 reduce-scatter.25
  1017.7 98.6 reduce-scatter.19
  1122.8 135.1 reduce-scatter.23
  1264.4 135.1 reduce-scatter.21
  1405.7 118.5 reduce-scatter.17
  1530.7 161.4 reduce-scatter.15
where the time goes:
time: 1710 us; the launch traced here: 1700 us
  waiting for transfers between devices  883 us (52%)
  matrix products  282 us (16%)
  blocking collectives  269 us (16%)
  other arithmetic  146 us (9%)
  local copies, waits for them, and re-layouts  84.7 us (5%)
  starting transfers between devices  18.7 us (1%)
    reduce_scatter x1, waiting for transfers between devices, local(): lax.psum_scatter(grad_ada_weight, ('dp', 'rows'), scatter_dimension=0, ti...  168 us
    reduce_scatter x1, waiting for transfers between devices, local(): lax.psum_scatter(grad_up_weight, ('dp', 'rows'), scatter_dimension=0, til...  142 us
    reduce_scatter x1, waiting for transfers between devices, local(): lax.psum_scatter(grad_down, ('dp', 'rows'), scatter_dimension=0, tiled=True)  141 us
    reduce_scatter x1, waiting for transfers between devices, local(): lax.psum_scatter(grad_qkv_weight, ('dp', 'rows'), scatter_dimension=0, ti...  125 us
    all_gather x1, blocking collectives, local(): lax.all_gather(ffn_kernel, ('dp', 'rows'), axis=1, tiled=True)  101 us
    unnamed x2, blocking collectives  83.8 us
    dot_general x5, matrix products, contract_cols(): lax.dot_general(left, right, (((1,), (1,)), ((), ())), preferred_element_...  69.1 us
    all_gather x1, blocking collectives, local(): lax.all_gather(attn_kernel, ('dp', 'rows'), axis=1, tiled=True)  68 us
  transfers between devices with their start and end apart: 23, of which 17 were waited for; matrix products, arithmetic and copies ran while one was open for 21% of the time, Pallas kernels for 0%

commit v1 on v0

--- a/solution.py
+++ b/solution.py
@@ -1,6 +1,10 @@
+import functools
+
 import jax
 import jax.numpy as jnp
 from jax import lax
+from jax.experimental import pallas as pl
+from jax.experimental.pallas import tpu as pltpu
 from jax.sharding import PartitionSpec as P
 
 PER_GROUP_WIDTH = 64
@@ -343,9 +347,580 @@
     return (layer_out, token_grad, derivative_of_context) + tuple(summed_grads)
 
 
+F32=jnp.float32; BF=jnp.bfloat16
+NT=(((1,),(1,)),((),()))
+TN=(((0,),(0,)),((),()))
+
+def head_masks(labels):
+    cells=labels.shape[0]
+    lane=lax.broadcasted_iota(jnp.int32,(cells,128),1)%64
+    lab=labels[:,None]
+    qm=(lane==lab).astype(BF)
+    km=jnp.where((lane!=lab)&(lane<4),-1e30,0.0).astype(BF)
+    return qm,km
+
+def attn_fwd_kernel(q_ref,k_ref,v_ref,qm_ref,km_ref,o_ref,lse_ref,*,scale,qb):
+    p=pl.program_id(0)
+    cells=q_ref.shape[0]
+    nq=cells//qb
+    lane=lax.broadcasted_iota(jnp.int32,(1,128),1)
+    @pl.when(p==0)
+    def _():
+        lse_ref[...]=jnp.zeros_like(lse_ref)
+    for h in range(2):
+        mine=(lane//64)==h
+        k=jnp.where(mine,k_ref[...],km_ref[...])
+        def body(i,c):
+            rows=pl.ds(pl.multiple_of(i*qb,qb),qb)
+            q=jnp.where(mine,q_ref[rows,:]*jnp.asarray(scale,BF),qm_ref[rows,:])
+            s=lax.dot_general(q,k,NT,preferred_element_type=F32)
+            m=jnp.max(s,axis=1,keepdims=True)
+            e=jnp.exp(s-m)
+            l=jnp.sum(e,axis=1,keepdims=True)
+            a=(e*(1.0/l)).astype(BF)
+            o=lax.dot_general(a,v_ref[...],(((1,),(0,)),((),())),preferred_element_type=F32).astype(BF)
+            if h==0:
+                o_ref[rows,:]=o
+            else:
+                o_ref[rows,:]=jnp.where(mine,o,o_ref[rows,:])
+            lse_ref[rows,:]=jnp.where(lane==2*p+h,m+jnp.log(l),lse_ref[rows,:])
+            return c
+        lax.fori_loop(0,nq,body,0)
+
+def attn_fwd(projected,qm,km,features,qb=256):
+    cells=projected.shape[0]
+    pairs=features//128
+    blk=lambda off: pl.BlockSpec((cells,128),lambda p: (0,off+p))
+    full=pl.BlockSpec((cells,128),lambda p:(0,0))
+    return pl.pallas_call(
+        functools.partial(attn_fwd_kernel,scale=0.125,qb=qb),
+        grid=(pairs,),
+        in_specs=[blk(0),blk(pairs),blk(2*pairs),full,full],
+        out_specs=[blk(0),full],
+        out_shape=[jax.ShapeDtypeStruct((cells,features),BF),jax.ShapeDtypeStruct((cells,128),F32)],
+        compiler_params=pltpu.CompilerParams(dimension_semantics=("arbitrary",),vmem_limit_bytes=60<<20),
+        name="attn_fwd",
+    )(projected,projected,projected,qm,km)
+
+def attn_bwd_kernel(q_ref,k_ref,v_ref,do_ref,o_ref,qm_ref,km_ref,lse_ref,dq_ref,dk_ref,dv_ref,qs,dqt,*,scale,kb):
+    p=pl.program_id(0)
+    cells=q_ref.shape[0]
+    nk=cells//kb
+    lane=lax.broadcasted_iota(jnp.int32,(1,128),1)
+    sub=lax.broadcasted_iota(jnp.int32,(128,1),0)
+    prod=do_ref[...].astype(F32)*o_ref[...].astype(F32)
+    hi=prod.astype(BF); lo=(prod-hi.astype(F32)).astype(BF)
+    srow=lax.broadcasted_iota(jnp.int32,(8,128),0)
+    slane=lax.broadcasted_iota(jnp.int32,(8,128),1)
+    sel=(slane//64==srow).astype(BF)
+    delta=lax.dot_general(sel,hi,NT,preferred_element_type=F32)+lax.dot_general(sel,lo,NT,preferred_element_type=F32)
+    qs[...]=q_ref[...]*jnp.asarray(scale,BF)
+    for h in range(2):
+        mine=(lane//64)==h
+        q=jnp.where(mine,qs[...],qm_ref[...])
+        lse=lse_ref[pl.ds(2*p+h,1),:]
+        dl=delta[h:h+1,:]
+        dqt[...]=jnp.zeros_like(dqt)
+        def body(i,c):
+            rows=pl.ds(pl.multiple_of(i*kb,kb),kb)
+            kr=k_ref[rows,:]
+            k=jnp.where(mine,kr,km_ref[rows,:])
+            v=jnp.where(mine,v_ref[rows,:],jnp.zeros((),BF))
+            st=lax.dot_general(k,q,NT,preferred_element_type=F32)
+            pt=jnp.exp(st-lse)
+            dpt=lax.dot_general(v,do_ref[...],NT,preferred_element_type=F32)
+            ds=(pt*(dpt-dl)).astype(BF)
+            dv=lax.dot_general(pt.astype(BF),do_ref[...],(((1,),(0,)),((),())),preferred_element_type=F32).astype(BF)
+            dk=lax.dot_general(ds,qs[...],(((1,),(0,)),((),())),preferred_element_type=F32).astype(BF)
+            dqt[...]+=lax.dot_general(kr,ds,TN,preferred_element_type=F32)
+            if h==0:
+                dv_ref[rows,:]=dv
+                dk_ref[rows,:]=dk
+            else:
+                dv_ref[rows,:]=jnp.where(mine,dv,dv_ref[rows,:])
+                dk_ref[rows,:]=jnp.where(mine,dk,dk_ref[rows,:])
+            return c
+        lax.fori_loop(0,nk,body,0)
+        dq=(jnp.transpose(dqt[...])*scale).astype(BF)
+        if h==0:
+            dq_ref[...]=dq
+        else:
+            dq_ref[...]=jnp.where(mine,dq,dq_ref[...])
+
+def attn_bwd(projected,dout,out,qm,km,lse_t,features,kb=256):
+    cells=projected.shape[0]
+    pairs=features//128
+    blk=lambda off: pl.BlockSpec((cells,128),lambda p: (0,off+p))
+    full=pl.BlockSpec((cells,128),lambda p:(0,0))
+    o=jax.ShapeDtypeStruct((cells,features),BF)
+    return pl.pallas_call(
+        functools.partial(attn_bwd_kernel,scale=0.125,kb=kb),
+        grid=(pairs,),
+        in_specs=[blk(0),blk(pairs),blk(2*pairs),blk(0),blk(0),full,full,pl.BlockSpec((128,cells),lambda p:(0,0))],
+        out_specs=[blk(0),blk(0),blk(0)],
+        out_shape=[o,o,o],
+        scratch_shapes=[pltpu.VMEM((cells,128),BF),pltpu.VMEM((128,cells),F32)],
+        compiler_params=pltpu.CompilerParams(dimension_semantics=("arbitrary",),vmem_limit_bytes=60<<20),
+        name="attn_bwd",
+    )(projected,projected,projected,dout,out,qm,km,lse_t)
+
+MESH=pl.DeviceIdType.MESH
+NZ,NC,NR=4,2,4
+
+
+def here():
+    dp=lax.axis_index("dp"); rows=lax.axis_index("rows")
+    return dp//NC, lax.rem(dp,NC), rows
+
+
+def dev(z,core,rows):
+    return (z*NC+core, rows)
+
+
+def partner_xy(rows,t):
+    x=lax.rem(rows,2); y=rows//2
+    tx=t%2; ty=t//2
+    nx=1-x if tx else x
+    ny=1-y if ty else y
+    return ny*2+nx
+
+
+def rcopy(src,dst,ssem,rsem,target):
+    return pltpu.make_async_remote_copy(src_ref=src,dst_ref=dst,send_sem=ssem,recv_sem=rsem,device_id=target,device_id_type=MESH)
+
+
+def barrier_all():
+    dp=lax.axis_index("dp"); rows=lax.axis_index("rows")
+    me=dp*NR+rows
+    total=NZ*NC*NR
+    bar=pltpu.get_barrier_semaphore()
+    def body(k,c):
+        other=lax.rem(me+k,total)
+        pl.semaphore_signal(bar,inc=1,device_id=(other//NR,lax.rem(other,NR)),device_id_type=MESH)
+        return c
+    lax.fori_loop(1,total,body,0)
+    pl.semaphore_wait(bar,total-1)
+
+
+def zmod(v):
+    return lax.rem(v+NZ,NZ)
+
+
+class Gather:
+    SEMS=[(NZ,),(NZ,),(NZ,NR),(NZ,NR),(NZ,NR),(NZ,NR),(1,)]
+
+    def __init__(self,shard,full,sems):
+        self.shard,self.full=shard,full
+        self.sz,self.rz,self.sx,self.rx,self.sc,self.rc,self.lo=sems
+        self.z,self.core,self.rows=here()
+
+    def slot(self,dz,t,core):
+        rows=self.rows if t==0 else partner_xy(self.rows,t)
+        return self.full.at[zmod(self.z-dz),core,rows]
+
+    def zcopy(self,dz,receive=False):
+        dst=self.slot(dz if receive else 0,0,self.core)
+        return rcopy(self.shard,dst,self.sz.at[dz],self.rz.at[dz],dev(zmod(self.z+dz),self.core,self.rows))
+
+    def piece(self,dz):
+        return self.shard if dz==0 else self.slot(dz,0,self.core)
+
+    def xcopy(self,dz,t,receive=False):
+        dst=self.slot(dz,t if receive else 0,self.core)
+        return rcopy(self.piece(dz),dst,self.sx.at[dz,t],self.rx.at[dz,t],dev(self.z,self.core,partner_xy(self.rows,t)))
+
+    def ccopy(self,dz,t,receive=False):
+        src=self.piece(dz) if t==0 else self.slot(dz,t,self.core)
+        dst=self.slot(dz,t,1-self.core if receive else self.core)
+        return rcopy(src,dst,self.sc.at[dz,t],self.rc.at[dz,t],dev(self.z,1-self.core,self.rows))
+
+    def local(self):
+        return pltpu.make_async_copy(self.shard,self.slot(0,0,self.core),self.lo.at[0])
+
+    def start(self):
+        for dz in range(1,NZ):
+            self.zcopy(dz).start()
+        for t in range(1,NR):
+            self.xcopy(0,t).start()
+        self.ccopy(0,0).start()
+        self.local().start()
+
+    def zstep(self,dz):
+        self.zcopy(dz,True).wait_recv()
+        for t in range(1,NR):
+            self.xcopy(dz,t).start()
+        self.ccopy(dz,0).start()
+
+    def xstep(self,dz,t):
+        self.xcopy(dz,t,True).wait_recv()
+        self.ccopy(dz,t).start()
+
+    def finish(self):
+        for dz in range(NZ):
+            for t in range(NR):
+                self.ccopy(dz,t,True).wait_recv()
+        for dz in range(1,NZ):
+            self.zcopy(dz).wait_send()
+        for dz in range(NZ):
+            for t in range(NR):
+                if t: self.xcopy(dz,t).wait_send()
+                self.ccopy(dz,t).wait_send()
+        self.local().wait()
+
+    def run_z(self):
+        for dz in range(1,NZ): self.zstep(dz)
+
+    def run_x(self):
+        for dz in range(NZ):
+            for t in range(1,NR): self.xstep(dz,t)
+
+
+class Scatter:
+    SEMS=[(1,),(1,),(1,),(NR,),(NR,),(NZ,),(NZ,)]
+
+    @staticmethod
+    def scratch(r,c,dt):
+        return [pltpu.VMEM((NZ,NR,r,c),dt),pltpu.VMEM((NZ,NR,r,c),dt),pltpu.VMEM((NR,NZ,r,c),dt),pltpu.VMEM((NZ,r,c),dt),pltpu.VMEM((NZ,r,c),dt)]
+
+    def __init__(self,part,out,bufs,sems):
+        self.part,self.out=part,out
+        self.own,self.sib,self.xin,self.zout,self.zin=bufs
+        self.lo,self.sc,self.rc,self.sx,self.rx,self.sz,self.rz=sems
+        self.z,self.core,self.rows=here()
+        self.dt=self.own.dtype
+
+    def lcopy(self):
+        return pltpu.make_async_copy(self.part.at[:,self.core],self.own,self.lo.at[0])
+
+    def ccopy(self):
+        return rcopy(self.part.at[:,1-self.core],self.sib,self.sc.at[0],self.rc.at[0],dev(self.z,1-self.core,self.rows))
+
+    def xcopy(self,t):
+        to=partner_xy(self.rows,t)
+        return rcopy(self.own.at[:,to],self.xin.at[t],self.sx.at[t],self.rx.at[t],dev(self.z,self.core,to))
+
+    def zcopy(self,dz):
+        to=zmod(self.z+dz)
+        return rcopy(self.zout.at[to],self.zin.at[dz],self.sz.at[dz],self.rz.at[dz],dev(to,self.core,self.rows))
+
+    def start(self):
+        self.ccopy().start(); self.lcopy().start()
+
+    def cstep(self):
+        self.lcopy().wait(); self.ccopy().wait_recv()
+        def body(i,c):
+            a,b=i//NR,lax.rem(i,NR)
+            self.own[a,b]=(self.own[a,b].astype(F32)+self.sib[a,b].astype(F32)).astype(self.dt)
+            return c
+        lax.fori_loop(0,NZ*NR,body,0)
+        for t in range(1,NR): self.xcopy(t).start()
+
+    def xstep(self):
+        for t in range(1,NR): self.xcopy(t).wait_recv()
+        def body(a,c):
+            s=self.own[a,self.rows].astype(F32)
+            for t in range(1,NR): s=s+self.xin[t,a].astype(F32)
+            self.zout[a]=s.astype(self.dt)
+            return c
+        lax.fori_loop(0,NZ,body,0)
+        for dz in range(1,NZ): self.zcopy(dz).start()
+
+    def zstep(self):
+        for dz in range(1,NZ): self.zcopy(dz).wait_recv()
+        s=self.zout[self.z].astype(F32)
+        for dz in range(1,NZ): s=s+self.zin[dz].astype(F32)
+        self.out[...]=s
+
+    def finish(self):
+        self.ccopy().wait_send()
+        for t in range(1,NR): self.xcopy(t).wait_send()
+        for dz in range(1,NZ): self.zcopy(dz).wait_send()
+
+
+class Swap:
+    SEMS=[(NR,),(NR,),(1,)]
+    def __init__(self,src,dst,sems):
+        self.src,self.dst=src,dst
+        self.s,self.r,self.lo=sems
+        self.z,self.core,self.rows=here()
+    def copy(self,t,receive=False):
+        to=partner_xy(self.rows,t)
+        return rcopy(self.src.at[to],self.dst.at[to if receive else self.rows],self.s.at[t],self.r.at[t],dev(self.z,self.core,to))
+    def local(self):
+        return pltpu.make_async_copy(self.src.at[self.rows],self.dst.at[self.rows],self.lo.at[0])
+    def start(self):
+        for t in range(1,NR): self.copy(t).start()
+        self.local().start()
+    def wait(self):
+        for t in range(1,NR): self.copy(t,True).wait_recv()
+        self.local().wait()
+    def finish(self):
+        for t in range(1,NR): self.copy(t).wait_send()
+
+
+class AllToAll:
+    N=NZ*NC*NR
+    SEMS=[(N,),(N,),(1,)]
+    def __init__(self,src,dst,sems,one=False):
+        self.src,self.dst,self.one=src,dst,one
+        self.s,self.r,self.lo=sems
+        self.me=lax.axis_index("dp")*NR+lax.axis_index("rows")
+    def piece(self,n):
+        return self.src if self.one else self.src.at[n]
+    def copy(self,k,receive=False):
+        to=lax.rem(self.me+k,self.N)
+        frm=lax.rem(self.me-k+self.N,self.N)
+        return rcopy(self.piece(to),self.dst.at[frm if receive else self.me],self.s.at[k],self.r.at[k],(to//NR,lax.rem(to,NR)))
+    def local(self):
+        return pltpu.make_async_copy(self.piece(self.me),self.dst.at[self.me],self.lo.at[0])
+    def each(self,fn):
+        def body(k,c):
+            fn(k); return c
+        lax.fori_loop(1,self.N,body,0)
+    def start(self):
+        self.each(lambda k:self.copy(k).start())
+        self.local().start()
+    def wait(self):
+        self.each(lambda k:self.copy(k,True).wait_recv())
+        self.local().wait()
+    def finish(self):
+        self.each(lambda k:self.copy(k).wait_send())
+
+
+def sem_types(shapes):
+    return [pltpu.SemaphoreType.DMA(s) for s in shapes]
+HBM=pl.BlockSpec(memory_space=pl.ANY)
+VM=pl.BlockSpec(memory_space=pltpu.VMEM)
+NDEV=NZ*NC*NR
+
+
+def enter_kernel(n_w,*refs):
+    it=iter(refs)
+    tok,cot,cond,ada,bias=[next(it) for _ in range(5)]
+    shards=[next(it) for _ in range(n_w)]
+    tok_o,cot_o,cond_o,mod_o=[next(it) for _ in range(4)]
+    fulls=[next(it) for _ in range(n_w)]
+    condv,part,modin=[next(it) for _ in range(3)]
+    take=lambda cls:[next(it) for _ in cls.SEMS]
+    barrier_all()
+    c_all=AllToAll(cond,condv,take(AllToAll),one=True)
+    swap_t=Swap(tok,tok_o,take(Swap))
+    swap_c=Swap(cot,cot_o,take(Swap))
+    m_all=AllToAll(part,modin,take(AllToAll))
+    gathers=[Gather(s,f,take(Gather)) for s,f in zip(shards,fulls)]
+    c_all.start()
+    swap_t.start()
+    gathers[0].start()
+    c_all.wait()
+    me=c_all.me
+    feats=ada.shape[0]
+    cv=condv[:,0,:].astype(F32)
+    low=(cv/(1.0+jnp.exp(-cv))).astype(BF)
+    width=cv.shape[1]
+    pick=(lax.broadcasted_iota(jnp.int32,(width,feats),0)==lax.broadcasted_iota(jnp.int32,(width,feats),1)+feats*me).astype(BF)
+    mine=jnp.dot(low,pick,preferred_element_type=F32).astype(BF)
+    chunk=768
+    for c in range(ada.shape[1]//chunk):
+        pr=jnp.dot(mine,ada[:,c*chunk:(c+1)*chunk],preferred_element_type=F32)
+        for l in range(chunk//128):
+            i=c*(chunk//128)+l
+            part[:,i,:]=pr[:,l*128:(l+1)*128]+bias[i:i+1,:]
+    cond_o[...]=low
+    m_all.start()
+    gathers[0].run_z()
+    for g in gathers[1:]: g.start()
+    m_all.wait()
+    s=modin[0]
+    def add(i,s): return s+modin[i]
+    mod_o[...]=lax.fori_loop(1,NDEV,add,s)
+    swap_t.wait()
+    gathers[0].run_x()
+    for g in gathers[1:]:
+        g.run_z()
+    swap_c.start()
+    for g in gathers[1:]:
+        g.run_x()
+    swap_c.wait()
+    for g in gathers: g.finish()
+    swap_t.finish(); swap_c.finish(); c_all.finish(); m_all.finish()
+
+
+def enter(tok,cot,cond_row,ada,bias_rows,shards):
+    n_w=len(shards)
+    scr=[pltpu.VMEM((NDEV,)+cond_row.shape,cond_row.dtype),pltpu.VMEM((NDEV,)+bias_rows.shape,F32),pltpu.VMEM((NDEV,)+bias_rows.shape,F32)]
+    sems=sem_types(AllToAll.SEMS)+sem_types(Swap.SEMS)*2+sem_types(AllToAll.SEMS)+sem_types(Gather.SEMS)*n_w
+    outs=[jax.ShapeDtypeStruct(tok.shape,tok.dtype),jax.ShapeDtypeStruct(cot.shape,cot.dtype),
+          jax.ShapeDtypeStruct((NDEV,cond_row.shape[1]),BF),jax.ShapeDtypeStruct(bias_rows.shape,F32)]
+    outs+=[jax.ShapeDtypeStruct((NZ,NC,NR)+s.shape,s.dtype) for s in shards]
+    return pl.pallas_call(
+        functools.partial(enter_kernel,n_w),
+        in_specs=[HBM,HBM,HBM,VM,VM]+[HBM]*n_w,
+        out_specs=[HBM,HBM,VM,VM]+[HBM]*n_w,
+        out_shape=outs,
+        scratch_shapes=scr+sems,
+        compiler_params=pltpu.CompilerParams(collective_id=0,has_side_effects=True,vmem_limit_bytes=48<<20),
+        name="enter",
+    )(tok,cot,cond_row,ada,bias_rows,*shards)
+
+
+def leave_kernel(n_g,refs_spec,*refs):
+    it=iter(refs)
+    lay,tg,gm,low,ada=[next(it) for _ in range(5)]
+    parts=[next(it) for _ in range(n_g)]
+    lay_o,tg_o,ctx_o,adag_o,gm_o=[next(it) for _ in range(5)]
+    gouts=[next(it) for _ in range(n_g)]
+    gmv,ctxs,ctxv=[next(it) for _ in range(3)]
+    bufs=[[next(it) for _ in range(5)] for _ in range(n_g)]
+    take=lambda cls:[next(it) for _ in cls.SEMS]
+    barrier_all()
+    g_all=AllToAll(gm,gmv,take(AllToAll),one=True)
+    x_all=AllToAll(ctxs,ctxv,take(AllToAll))
+    sl=Swap(lay,lay_o,take(Swap)); st=Swap(tg,tg_o,take(Swap))
+    sc=[Scatter(p,o,b,take(Scatter)) for p,o,b in zip(parts,gouts,bufs)]
+    g_all.start()
+    for s in sc: s.start()
+    st.start(); sl.start()
+    g_all.wait()
+    me=g_all.me
+    feats=ada.shape[0]
+    width=low.shape[1]
+    pick=(lax.broadcasted_iota(jnp.int32,(width,feats),0)==lax.broadcasted_iota(jnp.int32,(width,feats),1)+feats*me).astype(BF)
+    mine=jnp.dot(low[...],pick,preferred_element_type=F32).astype(BF)
+    acc=jnp.zeros((gmv.shape[0],feats),F32)
+    for i in range(gmv.shape[1]):
+        g=gmv[:,i,:]
+        adag_o[:,i*128:(i+1)*128]=lax.dot_general(mine,g,(((0,),(0,)),((),())),preferred_element_type=F32)
+        acc=acc+lax.dot_general(g,ada[:,i*128:(i+1)*128],(((1,),(1,)),((),())),preferred_element_type=F32)
+    gm_o[...]=jnp.sum(gmv[...].astype(F32),axis=0)
+    for n in range(NDEV):
+        g0=(n//NR)*NR
+        ctxs[n,0:NR,0:feats]=acc[g0:g0+NR,:]
+    x_all.start()
+    for s in sc: s.cstep()
+    x_all.wait()
+    ctx_o[...]=ctxv[...]
+    for s in sc: s.xstep()
+    for s in sc: s.zstep()
+    st.wait(); sl.wait()
+    for s in sc: s.finish()
+    st.finish(); sl.finish(); g_all.finish(); x_all.finish()
+
+
+def leave(lay,tg,gm,low,ada,parts):
+    n_g=len(parts)
+    cols=ada.shape[1]
+    scr=[pltpu.VMEM((NDEV,)+gm.shape,gm.dtype),pltpu.VMEM((NDEV,8,128),F32),pltpu.VMEM((NDEV,8,128),F32)]
+    for p in parts: scr+=Scatter.scratch(p.shape[3],p.shape[4],p.dtype)
+    sems=sem_types(AllToAll.SEMS)*2+sem_types(Swap.SEMS)*2+sem_types(Scatter.SEMS)*n_g
+    outs=[jax.ShapeDtypeStruct(lay.shape,lay.dtype),jax.ShapeDtypeStruct(tg.shape,tg.dtype),
+          jax.ShapeDtypeStruct((NDEV,8,128),F32),jax.ShapeDtypeStruct(ada.shape,F32),jax.ShapeDtypeStruct(gm.shape,F32)]
+    outs+=[jax.ShapeDtypeStruct(p.shape[3:],F32) for p in parts]
+    return pl.pallas_call(
+        functools.partial(leave_kernel,n_g,None),
+        in_specs=[HBM,HBM,HBM,VM,VM]+[HBM]*n_g,
+        out_specs=[HBM,HBM,VM,VM,VM]+[VM]*n_g,
+        out_shape=outs,
+        scratch_shapes=scr+sems,
+        compiler_params=pltpu.CompilerParams(collective_id=1,has_side_effects=True,vmem_limit_bytes=60<<20),
+        name="leave",
+    )(lay,tg,gm,low,ada,*parts)
+
+
+def own_rows(padded_cells):
+    return jnp.pad(padded_cells,((0,0),(1,1),(1,1),(0,0)))
+
+
+def fast(tokens,conditioning,item_map,ada_weight,ada_bias,attn_kernel,qkv_weight,out_weight,up_weight,ffn_kernel,down_weight,out_cotangent):
+    canvases,rows_here,cols,features=tokens.shape
+    side=rows_here*NR
+    cells=side*cols
+    rows=lax.axis_index("rows"); dp=lax.axis_index("dp"); me=dp*NR+rows
+    hidden=up_weight.shape[1]
+    cond_row=lax.dynamic_slice_in_dim(conditioning,rows,1,0)
+    cond_row8=jnp.pad(cond_row,((0,7),(0,0)))
+    mod_cols=ada_weight.shape[1]
+    bshard=ada_bias.shape[0]
+    bias_rows=lax.dynamic_update_slice_in_dim(jnp.zeros((mod_cols,),F32),ada_bias.astype(F32),me*bshard,0).reshape(mod_cols//128,128)
+    pad8=(-(mod_cols//128))%8
+    taps=jnp.pad(jnp.concatenate([attn_kernel,ffn_kernel],axis=1),((0,7),(0,128-attn_kernel.shape[1]-ffn_kernel.shape[1])))
+    ta,tf=attn_kernel.shape[1],ffn_kernel.shape[1]
+    tok,cot,low_all,mod,qkv_f,taps_f,out_f,up_f,down_f=enter(
+        tokens.reshape(NR,rows_here*cols,features),out_cotangent.reshape(NR,rows_here*cols,features),
+        cond_row8,ada_weight,bias_rows,[qkv_weight,taps,out_weight,up_weight,down_weight])
+    full2=lambda a:a.reshape(-1,a.shape[-1])
+    triple_full,out_full,up_full,down_full=full2(qkv_f),full2(out_f),full2(up_f),full2(down_f)
+    taps_f=taps_f.reshape(NDEV,16,128)[:,:9]
+    kernel_attn=taps_f[:,:,:ta].transpose(1,0,2).reshape(9,features)
+    kernel_ffn=taps_f[:,:,ta:ta+tf].transpose(1,0,2).reshape(9,hidden)
+    labels=lax.dynamic_slice_in_dim(item_map,rows,1,0)
+    labels_pad=jnp.pad(labels,((0,0),(1,1),(1,1)),constant_values=-1)
+    shift1,scale1,gate1,shift2,scale2,gate2=(mod.reshape(6,features)[i][None,None,None] for i in range(6))
+    x=tok.reshape(1,side,cols,features).astype(F32)
+    incoming=cot.reshape(1,side,cols,features).astype(F32)
+    n1,i1=normalize(x)
+    m1=(n1*(1.0+scale1)+shift1).astype(BF)
+    m1p=own_rows(m1)
+    mix=conv_forward(m1p,labels_pad,labels,kernel_attn).astype(BF).reshape(cells,features)
+    projected=jnp.dot(mix,triple_full,preferred_element_type=F32).astype(BF)
+    qm,km=head_masks(labels.reshape(cells))
+    attended,lse=attn_fwd(projected,qm,km,features)
+    branch=jnp.dot(attended,out_full,preferred_element_type=F32).reshape(x.shape)
+    middle=x+gate1*branch
+    n2,i2=normalize(middle)
+    m2=(n2*(1.0+scale2)+shift2).astype(BF)
+    m2r=m2.reshape(cells,features)
+    hid=jnp.dot(m2r,up_full,preferred_element_type=F32).astype(BF).reshape(1,side,cols,hidden)
+    hidp=own_rows(hid)
+    pre=conv_forward(hidp,labels_pad,labels,kernel_ffn)
+    act,gback=jax.vjp(jax.nn.gelu,pre)
+    glow=act.astype(BF).reshape(cells,hidden)
+    fbranch=jnp.dot(glow,down_full,preferred_element_type=F32).reshape(x.shape)
+    layer_out=(middle+gate2*fbranch).astype(BF)
+    g_gate2=jnp.sum(incoming*fbranch,axis=(1,2))
+    gffn=(gate2*incoming).astype(BF).reshape(cells,features)
+    g_down=contract_rows(glow,gffn)
+    ggelu=contract_cols(gffn,down_full).reshape(1,side,cols,hidden)
+    gpre=gback(ggelu)[0].astype(BF)
+    gprep=own_rows(gpre)
+    g_kffn=kernel_grad(gpre,hidp,labels_pad,labels)
+    gup=conv_mirror(gprep,labels_pad,labels,kernel_ffn).astype(BF).reshape(cells,hidden)
+    g_up=contract_rows(m2r,gup)
+    gm2=contract_cols(gup,up_full).reshape(x.shape)
+    g_scale2=jnp.sum(gm2*n2,axis=(1,2)); g_shift2=jnp.sum(gm2,axis=(1,2))
+    gmid=incoming+normalize_back(gm2*(1.0+scale2),n2,i2)
+    g_gate1=jnp.sum(gmid*branch,axis=(1,2))
+    gattn=(gate1*gmid).astype(BF).reshape(cells,features)
+    g_out=contract_rows(attended,gattn)
+    gatt=contract_cols(gattn,out_full).astype(BF)
+    dq,dk,dv=attn_bwd(projected,gatt,attended,qm,km,lse.T,features)
+    gproj=jnp.concatenate([dq,dk,dv],axis=1)
+    g_qkv=contract_rows(mix,gproj)
+    gmix=contract_cols(gproj,triple_full).astype(BF).reshape(x.shape)
+    g_kattn=kernel_grad(gmix,m1p,labels_pad,labels)
+    gm1=conv_mirror(own_rows(gmix),labels_pad,labels,kernel_attn)
+    g_scale1=jnp.sum(gm1*n1,axis=(1,2)); g_shift1=jnp.sum(gm1,axis=(1,2))
+    tgrad=gmid+normalize_back(gm1*(1.0+scale1),n1,i1)
+    gmod=jnp.concatenate([g_shift1,g_scale1,g_gate1,g_shift2,g_scale2,g_gate2],axis=-1).astype(BF)
+    gtaps=jnp.concatenate([g_kattn.reshape(9,NDEV,ta),g_kffn.reshape(9,NDEV,tf)],axis=2).transpose(1,0,2)
+    gtaps=jnp.pad(gtaps,((0,0),(0,7),(0,128-ta-tf))).reshape(NZ,NC,NR,16,128)
+    sp=lambda g:g.astype(BF).reshape(NZ,NC,NR,g.shape[0]//NDEV,g.shape[1])
+    lay,tg,ctx,adag,gmsum,q_o,t_o,o_o,u_o,d_o=leave(
+        layer_out.reshape(NR,rows_here*cols,features),tgrad.astype(BF).reshape(NR,rows_here*cols,features),
+        gmod.reshape(mod_cols//128,128),low_all,ada_weight,[sp(g_qkv),gtaps,sp(g_out),sp(g_up),sp(g_down)])
+    shape4=(NR,rows_here,cols,features)
+    feats=ada_weight.shape[0]
+    dsilu=ctx[:,:NR,:feats].transpose(1,0,2).reshape(NR,features)
+    cv=conditioning.astype(F32)
+    _,sback=jax.vjp(jax.nn.silu,cv)
+    dctx=sback(dsilu)[0]
+    gbias=lax.dynamic_slice_in_dim(gmsum.reshape(mod_cols),me*bshard,bshard,0)
+    return (lay.reshape(shape4),tg.reshape(shape4).astype(F32),dctx,adag,gbias,t_o[:9,:ta],q_o,o_o,u_o,t_o[:9,ta:ta+tf],d_o)
+
+
 def solution(mesh):
+    quick=dict(mesh.shape)=={"dp":NZ*NC,"rows":NR}
     return jax.shard_map(
-        local,
+        fast if quick else local,
         mesh=mesh,
         in_specs=(
             P("dp", "rows", None, None),

time: 1710 us -> 662 us (0.39)
  waiting for transfers between devices: 883 us -> 0 us
  Pallas kernels: 0 us -> 362 us
  blocking collectives: 269 us -> 0 us
  matrix products: 282 us -> 121 us
  local copies, waits for them, and re-layouts: 84.7 us -> 32.5 us
  starting transfers between devices: 18.7 us -> 0 us
    reduce_scatter x7 -> x0, waiting for transfers between devices: 630 us -> none  [the longest x1 168 us: local(): lax.psum_scatter(grad_ada_weight, ('dp', 'rows'), scatter_dimension=0, ti...]
    pallas_call x0 -> x4, Pallas kernels: none -> 362 us  [the longest x1 139 us: leave(): pl.pallas_call(functools.partial(leave_kernel, n_g, None), in_specs=[HBM,...]
    all_gather x7 -> x0, waiting for transfers between devices: 173 us -> none  [the longest x1 60.1 us: local(): lax.all_gather(key_rows, 'rows', axis=1, tiled=True)]
    all_gather x2 -> x0, blocking collectives: 169 us -> none  [the longest x1 101 us: local(): lax.all_gather(ffn_kernel, ('dp', 'rows'), axis=1, tiled=True)]
    dot_general x10 -> x4, matrix products: 145 us -> 26.2 us  [the longest x1 8.66 us: fast(): jnp.dot(glow, down_full, preferred_element_type=F32).reshape(x.shape)]
    unnamed x2 -> x0, blocking collectives: 83.8 us -> none
    ppermute x8 -> x0, waiting for transfers between devices: 46.7 us -> none  [the longest x4 28 us: padded(): lax.ppermute(lax.slice_in_dim(block, 0, width, axis=dim), axis, backward)]
    convert_element_type x7 -> x9, other arithmetic: 73.9 us -> 115 us  [the longest x1 43.9 us: fast(): glow = act.astype(BF).reshape(cells, hidden)]
  transfers between devices with their start and end apart: 23 -> 0, of which waited for: 17 -> 0; matrix products, arithmetic and copies ran while one was open for 21% -> 0% of each run, Pallas kernels for 0% -> 0%
where the time goes in v1:
time: 662 us; the launch traced here: 653 us
  Pallas kernels  362 us (55%)
  other arithmetic  134 us (20%)
  matrix products  121 us (18%)
  local copies, waits for them, and re-layouts  32.5 us (5%)
    pallas_call x1, Pallas kernels, leave(): pl.pallas_call(functools.partial(leave_kernel, n_g, None), in_specs=[HBM,...  139 us
    pallas_call x1, Pallas kernels, enter(): pl.pallas_call(functools.partial(enter_kernel, n_w), in_specs=[HBM, HBM,...  136 us
    dot_general x4, matrix products, contract_cols(): lax.dot_general(left, right, (((1,), (1,)), ((), ())), preferred_element_...  70.4 us
    pallas_call x1, Pallas kernels, attn_bwd(): pl.pallas_call(functools.partial(attn_bwd_kernel, scale=0.125, kb=kb), gr...  46.2 us
    convert_element_type x1, other arithmetic, fast(): glow = act.astype(BF).reshape(cells, hidden)  43.9 us
    pallas_call x1, Pallas kernels, attn_fwd(): pl.pallas_call(functools.partial(attn_fwd_kernel, scale=0.125, qb=qb), gr...  41.6 us
    convert_element_type x1, other arithmetic, fast(): conv_mirror(gprep, labels_pad, labels, kernel_ffn).astype(BF)  39.9 us
    dot_general x4, matrix products, contract_rows(): lax.dot_general(left, right, (((0,), (0,)), ((), ())), preferred_element_...  24.9 us

profile of v1, /device:TPU:0, one launch (start us, length us, event | category | flops | bytes accessed | tf_op | source)
XLA Modules:
  0.0 653.2 jit_solution(5994990269470417431)
XLA Ops:
  7.4 135.7 %enter.1 = (bf16[4,256,768]{2,1,0:T(8,128)(2,1)S(1)}, bf16[4,256,768]{2,1,0:T(8,128)(2,1)S(1)}, bf16[32,768]{1,0:T(8,128)(2,1)S(1)}, f32[36,128]{1,0:T(8,128)S(1...) custom-call(bf16[4,256,768]{2,1,0:T(8,128)(2,1)} %bitcast.192, ...), custom_call_target="tpu_custom_call" | custom-call | tf_op jit(solution)/shard_map/enter/pallas_call | solution.py:755
  147.2 2.8 add_convert_fusion.4
  151.1 12.8 %fusion.66 = bf16[1,32,32,768]{3,2,1,0:T(8,128)(2,1)S(1)} fusion(bf16[1,32,32,768]{3,2,1,0:T(8,128)(2,1)} %get-tuple-element.98, f32[768]{0:T(1024)S(1)} %reshape.986, f32[768]{0:T(1024)S(1)} %reshape.985, f32[768]{0:T(1024)S(1)} %reshape.984, f32[768]{0:T(1024)S(1)} %reshape.983, f32[768]{0:T(1024)S(1)} %reshape.982, f32[768]{0:T(1024)S(1)} %reshape.981, ...), kind=kLoop, calls=%fused_computation.124 | loop fusion | flops 27525120 | bytes 3181568 | tf_op jit(solution)/shard_map/convert_element_type | solution.py:863
  164.0 1.1 copy-done.28
  165.1 7.4 %convolution_convert_fusion.q_ref.k_ref.v_ref = bf16[1024,2304]{1,0:T(8,128)(2,1)} fusion(bf16[1024,768]{1,0:T(8,128)(2,1)S(1)} %bitcast.194, bf16[768,2304]{1,0:T(8,128)(2,1)} %bitcast.218), kind=kOutput, calls=%fused_computation.104 | convolution fusion | flops 3626237952 | bytes 9830400 | tf_op jit(solution)/shard_map/dot_general | solution.py:864
  174.5 41.6 %attn_fwd.1 = (bf16[1024,768]{1,0:T(8,128)(2,1)}, f32[1024,128]{1,0:T(8,128)}) custom-call(bf16[1024,2304]{1,0:T(8,128)(2,1)} %convolution_convert_fusion.q_ref.k_ref.v_ref, bf16[1024,2304]{1,0:T(8,128)(2,1)} %convolution_convert_fusion.q_ref.k_ref.v_ref, bf16[1024,2304]{1,0:T(8,128)(2,1)} %convolution_convert_fusion.q_ref.k_ref.v_ref, ...), custom_call_target="tpu_custom_call" | custom-call | tf_op jit(solution)/shard_map/attn_fwd/pallas_call | solution.py:395
  216.0 3.1 fusion.151
  221.4 1.6 slice-done.3
  223.6 6.9 %convolution_convert_fusion.1 = bf16[1024,3072]{1,0:T(8,128)(2,1)} fusion(bf16[768,3072]{1,0:T(8,128)(2,1)S(1)} %bitcast.215, f32[1024,768]{1,0:T(8,128)S(1)} %fusion.99, f32[768]{0:T(1024)S(1)} %get-tuple-element.113, f32[768]{0:T(1024)S(1)} %get-tuple-element.114), kind=kOutput, calls=%fused_computation.105 | convolution fusion | flops 4837343232 | bytes 14161920 | tf_op jit(solution)/shard_map/dot_general | solution.py:872
  231.7 43.9 %multiply_convert_fusion = (bf16[1,32,32,3072]{3,2,1,0:T(8,128)(2,1)}, f32[1,32,32,3072]{3,2,1,0:T(8,128)}) fusion(f32[3072]{0:T(1024)S(1)} %reshape.996, pred[32,32]{1,0:T(8,128)(4,1)S(1)} %get-tuple-element.119, f32[3072]{0:T(1024)S(1)} %reshape.995, pred[32,32]{1,0:T(8,128)(4,1)S(1)} %get-tuple-element.120, f32[3072]{0:T(1024)S(1)} %reshape.994, ...), kind=kLoop, calls=%fused_computation.72 | loop fusion | flops 135266304 | bytes 25284608 | tf_op jit(solution)/shard_map/convert_element_type | solution.py:876
  275.6 8.7 %fusion.152 = f32[1024,768]{1,0:T(8,128)S(1)} fusion(bf16[1024,3072]{1,0:T(8,128)(2,1)} %bitcast.186, bf16[3072,768]{1,0:T(8,128)(2,1)} %bitcast.216), kind=kOutput, calls=%fused_computation.328 | convolution fusion | flops 4831838208 | bytes 14155776 | tf_op jit(solution)/shard_map/dot_general | solution.py:877
  284.4 3.0 add_convert_fusion
  287.4 2.5 copy-done.26
  289.9 6.9 %bitcast_convert_fusion = bf16[3072,768]{1,0:T(8,128)(2,1)} fusion(bf16[32,32,768]{2,1,0:T(8,128)(2,1)S(1)} %bitcast.199, bf16[1,32,32,3072]{3,2,1,0:T(8,128)(2,1)S(1)} %copy-done.26), kind=kOutput, calls=%fused_computation.73 | convolution fusion | flops 4834197504 | bytes 12582912 | tf_op jit(solution)/shard_map/dot_general | solution.py:106
  296.9 50.5 %fusion.45 = (f32[3072]{0:T(1024)S(1)}, f32[3072]{0:T(1024)S(1)}, f32[3072]{0:T(1024)S(1)}, f32[3072]{0:T(1024)S(1)}, f32[3072]{0:T(1024)S(1)}, /*index=5*/f32[3...) fusion(pred[32,32]{1,0:T(8,128)(4,1)S(1)} %get-tuple-element.119, ...), kind=kOutput, calls=%fused_computation.66 | convolution fusion | flops 5007971328 | bytes 37867520 | tf_op jit(solution)/shard_map/dot_general | solution.py:112
  347.4 39.9 %fusion.28 = bf16[1,32,32,3072]{3,2,1,0:T(8,128)(2,1)S(1)} fusion(bf16[1,32,32,3072]{3,2,1,0:T(8,128)(2,1)} %get-tuple-element.136, f32[3072]{0:T(1024)S(1)} %reshape.996, f32[3072]{0:T(1024)S(1)} %reshape.995, f32[3072]{0:T(1024)S(1)} %reshape.994, f32[3072]{0:T(1024)S(1)} %reshape.993, f32[3072]{0:T(1024)S(1)} %reshape.992, f32[3072]{0:T(1024)S(1)} %reshape.991, ...), kind=kLoop, calls=%fused_computation.49 | loop fusion | flops 110100480 | bytes 12701696 | tf_op jit(solution)/shard_map/convert_element_type | solution.py:886
  387.4 6.9 %bitcast_convert_fusion.1 = bf16[768,3072]{1,0:T(8,128)(2,1)} fusion(bf16[32,32,768]{2,1,0:T(8,128)(2,1)S(1)} %bitcast.198, bf16[1,32,32,3072]{3,2,1,0:T(8,128)(2,1)S(1)} %fusion.28), kind=kOutput, calls=%fused_computation.74 | convolution fusion | flops 4834197504 | bytes 12582912 | tf_op jit(solution)/shard_map/dot_general | solution.py:106
  394.3 8.2 %multiply_reduce_fusion.1 = (bf16[768]{0:T(1024)(128)(2,1)S(1)}, f32[1024]{0:T(1024)S(1)}, f32[1024]{0:T(1024)S(1)}, bf16[768]{0:T(1024)(128)(2,1)S(1)}, f32[1024,768]{1,0:T(8,128)S(1)}) fusion(f32[1024,768]{1,0:T(8,128)S(1)} %copy-done.19, f32[768]{0:T(1024)S(1)} %get-tuple-element.114, bf16[1024,3072]{1,0:T(8,128)(2,1)S(1)} %bitcast.182, ...), kind=kOutput, calls=%fused_computation.171 | convolution fusion | flops 4837339136 | bytes 17315840 | tf_op jit(solution)/shard_map/dot_general | solution.py:112
  402.5 1.9 multiply_reduce_fusion.2
  405.0 2.5 convolution_convert_fusion.5
  407.5 2.6 convolution_convert_fusion.4.do_ref
  411.1 46.2 %attn_bwd.1 = (bf16[1024,768]{1,0:T(8,128)(2,1)}, bf16[1024,768]{1,0:T(8,128)(2,1)}, bf16[1024,768]{1,0:T(8,128)(2,1)}) custom-call(bf16[1024,2304]{1,0:T(8,128)(2,1)} %convolution_convert_fusion.q_ref.k_ref.v_ref, bf16[1024,2304]{1,0:T(8,128)(2,1)} %convolution_convert_fusion.q_ref.k_ref.v_ref, ...), custom_call_target="tpu_custom_call" | custom-call | tf_op jit(solution)/shard_map/attn_bwd/pallas_call | solution.py:456
  457.3 1.7 constant_dynamic-update-slice_fusion.2
  461.8 9.2 %fusion.94 = (f32[768]{0:T(1024)S(1)}, f32[768]{0:T(1024)S(1)}, f32[768]{0:T(1024)S(1)}, f32[768]{0:T(1024)S(1)}, f32[768]{0:T(1024)S(1)}, /*index=5*/f32[768]{0...) fusion(pred[32,32]{1,0:T(8,128)(4,1)S(1)} %get-tuple-element.119, ...), kind=kOutput, calls=%fused_computation.152 | convolution fusion | flops 3650611200 | bytes 11436032 | tf_op jit(solution)/shard_map/dot_general | solution.py:112
  471.0 1.1 copy-done.24
  476.0 8.6 %convolution_convert_fusion.2 = bf16[768,2304]{1,0:T(8,128)(2,1)} fusion(bf16[1024,768]{1,0:T(8,128)(2,1)} %bitcast.195, bf16[1024,2304]{1,0:T(8,128)(2,1)} %copy-done.34), kind=kOutput, calls=%fused_computation.106 | convolution fusion | flops 3625648128 | bytes 9830400 | tf_op jit(solution)/shard_map/dot_general | solution.py:106
  484.8 9.5 %multiply_reduce_fusion.3 = (bf16[768]{0:T(1024)(128)(2,1)S(1)}, f32[32,32]{1,0:T(8,128)S(1)}, f32[32,32]{1,0:T(8,128)S(1)}, bf16[768]{0:T(1024)(128)(2,1)S(1)}, f32[1,32,32,768]{3,2,1,0:T(8,128)}) fusion(f32[1,32,32,768]{3,2,1,0:T(8,128)S(1)} %copy-done.17, f32[32,32]{1,0:T(8,128)S(1)} %copy-done.40, f32[32,32]{1,0:T(8,128)S(1)} %copy-done.42, ...), kind=kLoop, calls=%fused_computation.173 | loop fusion | flops 33812992 | bytes 7922688 | tf_op jit(solution)/shard_map/reduce_sum | solution.py:901
  495.3 6.7 %add_convert_fusion.1 = bf16[1,32,32,768]{3,2,1,0:T(8,128)(2,1)} fusion(f32[1,32,32,768]{3,2,1,0:T(8,128)} %get-tuple-element.99, f32[1,32,32,768]{3,2,1,0:T(8,128)} %bitcast.177, f32[1,32,32,768]{3,2,1,0:T(8,128)} %bitcast.180, f32[1,32,32,768]{3,2,1,0:T(8,128)} %get-tuple-element.95, f32[32,32]{1,0:T(8,128)S(1)} %broadcast_multiply_fusion, ...), kind=kLoop, calls=%fused_computation.174 | loop fusion | flops 15728640 | bytes 15770624 | tf_op jit(solution)/shard_map/convert_element_type | solution.py:908
  502.0 139.0 %leave.1 = (bf16[4,256,768]{2,1,0:T(8,128)(2,1)}, bf16[4,256,768]{2,1,0:T(8,128)(2,1)}, f32[32,8,128]{2,1,0:T(8,128)}, f32[24,4608]{1,0:T(8,128)}, f32[36,128]{1...) custom-call(bf16[4,256,768]{2,1,0:T(8,128)(2,1)} %get-tuple-element., ...), custom_call_target="tpu_custom_call" | custom-call | tf_op jit(solution)/shard_map/leave/pallas_call | solution.py:818
  641.1 3.6 convert.53
  645.5 1.3 dynamic_slice.11
  647.5 1.1 copy.58
  (281 shorter events, 32.4 us)
Async XLA Ops:
  0.6 150.3 %copy-start = (s32[4,32,32]{2,1,0:T(8,128)S(1)}, s32[4,32,32]{2,1,0:T(8,128)}, u32[]{:S(2)}) copy-start(s32[4,32,32]{2,1,0:T(8,128)} %param.14) | copy-start | bytes 49156
  144.7 139.6 %copy-start.2 = (bf16[4,256,768]{2,1,0:T(8,128)(2,1)}, bf16[4,256,768]{2,1,0:T(8,128)(2,1)S(1)}, u32[]{:S(2)}) copy-start(bf16[4,256,768]{2,1,0:T(8,128)(2,1)S(1)} %get-tuple-element.35) | copy-start | bytes 4718596
  144.7 139.6 %copy-start.4 = (bf16[4,256,768]{2,1,0:T(8,128)(2,1)}, bf16[4,256,768]{2,1,0:T(8,128)(2,1)S(1)}, u32[]{:S(2)}) copy-start(bf16[4,256,768]{2,1,0:T(8,128)(2,1)S(1)} %get-tuple-element.43) | copy-start | bytes 4718596
  147.2 137.1 %copy-start.44 = (f32[768]{0:T(1024)}, f32[768]{0:T(1024)S(1)}, u32[]{:S(2)}) copy-start(f32[768]{0:T(1024)S(1)} %get-tuple-element.117) | copy-start | bytes 9220
  150.2 22.3 %copy-start.51 = (f32[768]{0:T(1024)}, f32[768]{0:T(1024)S(1)}, u32[]{:S(2)}) copy-start(f32[768]{0:T(1024)S(1)} %reshape.977) | copy-start | bytes 9220
  150.3 22.2 %copy-start.53 = (f32[768]{0:T(1024)}, f32[768]{0:T(1024)S(1)}, u32[]{:S(2)}) copy-start(f32[768]{0:T(1024)S(1)} %reshape.979) | copy-start | bytes 9220
  150.4 22.1 %copy-start.55 = (f32[768]{0:T(1024)}, f32[768]{0:T(1024)S(1)}, u32[]{:S(2)}) copy-start(f32[768]{0:T(1024)S(1)} %reshape.980) | copy-start | bytes 9220
  150.5 22.0 %copy-start.57 = (f32[768]{0:T(1024)}, f32[768]{0:T(1024)S(1)}, u32[]{:S(2)}) copy-start(f32[768]{0:T(1024)S(1)} %reshape.981) | copy-start | bytes 9220
  150.6 22.0 %copy-start.59 = (f32[768]{0:T(1024)}, f32[768]{0:T(1024)S(1)}, u32[]{:S(2)}) copy-start(f32[768]{0:T(1024)S(1)} %reshape.982) | copy-start | bytes 9220
  150.7 21.9 %copy-start.61 = (f32[768]{0:T(1024)}, f32[768]{0:T(1024)S(1)}, u32[]{:S(2)}) copy-start(f32[768]{0:T(1024)S(1)} %reshape.983) | copy-start | bytes 9220
  150.8 21.8 %copy-start.63 = (f32[768]{0:T(1024)}, f32[768]{0:T(1024)S(1)}, u32[]{:S(2)}) copy-start(f32[768]{0:T(1024)S(1)} %reshape.984) | copy-start | bytes 9220
  150.9 21.7 %copy-start.65 = (f32[768]{0:T(1024)}, f32[768]{0:T(1024)S(1)}, u32[]{:S(2)}) copy-start(f32[768]{0:T(1024)S(1)} %reshape.985) | copy-start | bytes 9220
  151.0 21.6 %copy-start.67 = (f32[768]{0:T(1024)}, f32[768]{0:T(1024)S(1)}, u32[]{:S(2)}) copy-start(f32[768]{0:T(1024)S(1)} %reshape.986) | copy-start | bytes 9220
  219.7 64.7 %copy-start.49 = (f32[4,256]{1,0:T(4,128)}, f32[4,256]{1,0:T(4,128)S(1)}, u32[]{:S(2)}) copy-start(f32[4,256]{1,0:T(4,128)S(1)} %get-tuple-element.134) | copy-start | bytes 12292
  220.5 63.9 %copy-start.73 = (f32[4,256]{1,0:T(4,128)}, f32[4,256]{1,0:T(4,128)S(1)}, u32[]{:S(2)}) copy-start(f32[4,256]{1,0:T(4,128)S(1)} %get-tuple-element.131) | copy-start | bytes 12292
  221.3 9.2 %copy-start.18 = (f32[1024,768]{1,0:T(8,128)}, f32[1024,768]{1,0:T(8,128)S(1)}, u32[]{:S(2)}) copy-start(f32[1024,768]{1,0:T(8,128)S(1)} %fusion.99) | copy-start | bytes 9437188
  275.6 8.7 %copy-start.15 = (f32[1024,768]{1,0:T(8,128)S(1)}, f32[1024,768]{1,0:T(8,128)}, u32[]{:S(2)}) copy-start(f32[1024,768]{1,0:T(8,128)} %copy-done.14) | copy-start | bytes 9437188
  284.4 12.5 %slice-start = ((s8[12582912]{0:T(1024)(128)(4,1)}), s8[4194304]{0:T(1024)(128)(4,1)S(1)}, s32[]{:S(2)}) async-start(s8[12582912]{0:T(1024)(128)(4,1)} %bitcast.178), calls=%async_computation | async-start | bytes 8388608
  287.4 9.4 %copy-start.33 = (bf16[4,256,768]{2,1,0:T(8,128)(2,1)}, bf16[4,256,768]{2,1,0:T(8,128)(2,1)S(1)}, u32[]{:S(2)}) copy-start(bf16[4,256,768]{2,1,0:T(8,128)(2,1)S(1)} %get-tuple-element.126) | copy-start | bytes 4718596
  347.4 40.0 %copy-start.32 = (bf16[4,256,768]{2,1,0:T(8,128)(2,1)S(1)}, bf16[4,256,768]{2,1,0:T(8,128)(2,1)}, u32[]{:S(2)}) copy-start(bf16[4,256,768]{2,1,0:T(8,128)(2,1)} %get-tuple-element.100) | copy-start | bytes 4718596
  461.7 9.2 %copy-start.34 = (bf16[1024,2304]{1,0:T(8,128)(2,1)}, bf16[1024,2304]{1,0:T(8,128)(2,1)S(1)}, u32[]{:S(2)}) copy-start(bf16[1024,2304]{1,0:T(8,128)(2,1)S(1)} %constant_dynamic-update-slice_fusion) | copy-start | bytes 14155780
  461.7 9.2 %copy-start.78 = (f32[1,2,4,128]{3,2,1,0:T(4,128)S(1)}, f32[1,2,4,128]{3,2,1,0:T(4,128)}, u32[]{:S(2)}) copy-start(f32[1,2,4,128]{3,2,1,0:T(4,128)} %get-tuple-element.129) | copy-start | bytes 12292
  461.7 9.2 %copy-start.77 = (f32[1,2,4,128]{3,2,1,0:T(4,128)S(1)}, f32[1,2,4,128]{3,2,1,0:T(4,128)}, u32[]{:S(2)}) copy-start(f32[1,2,4,128]{3,2,1,0:T(4,128)} %get-tuple-element.127) | copy-start | bytes 12292
  461.7 10.4 %copy-start.3 = (bf16[4,256,768]{2,1,0:T(8,128)(2,1)S(1)}, bf16[4,256,768]{2,1,0:T(8,128)(2,1)}, u32[]{:S(2)}) copy-start(bf16[4,256,768]{2,1,0:T(8,128)(2,1)} %copy-done.2) | copy-start | bytes 4718596
  461.7 10.4 %copy-start.47 = (f32[768]{0:T(1024)S(1)}, f32[768]{0:T(1024)}, u32[]{:S(2)}) copy-start(f32[768]{0:T(1024)} %copy-done.46) | copy-start | bytes 9220
  461.7 10.3 %copy-start.70 = (f32[768]{0:T(1024)S(1)}, f32[768]{0:T(1024)}, u32[]{:S(2)}) copy-start(f32[768]{0:T(1024)} %copy-done.69) | copy-start | bytes 9220
  475.9 8.7 %copy-start.52 = (f32[768]{0:T(1024)S(1)}, f32[768]{0:T(1024)}, u32[]{:S(2)}) copy-start(f32[768]{0:T(1024)} %copy-done.51) | copy-start | bytes 9220
  476.0 8.7 %copy-start.54 = (f32[768]{0:T(1024)S(1)}, f32[768]{0:T(1024)}, u32[]{:S(2)}) copy-start(f32[768]{0:T(1024)} %copy-done.53) | copy-start | bytes 9220
  476.0 8.7 %copy-start.56 = (f32[768]{0:T(1024)S(1)}, f32[768]{0:T(1024)}, u32[]{:S(2)}) copy-start(f32[768]{0:T(1024)} %copy-done.55) | copy-start | bytes 9220
  484.8 10.4 %copy-start.74 = (f32[4,256]{1,0:T(4,128)S(1)}, f32[4,256]{1,0:T(4,128)}, u32[]{:S(2)}) copy-start(f32[4,256]{1,0:T(4,128)} %copy-done.73) | copy-start | bytes 12292
  484.8 10.5 %copy-start.50 = (f32[4,256]{1,0:T(4,128)S(1)}, f32[4,256]{1,0:T(4,128)}, u32[]{:S(2)}) copy-start(f32[4,256]{1,0:T(4,128)} %copy-done.49) | copy-start | bytes 12292
  641.1 11.7 %copy-start.1 = (s32[4,32,32]{2,1,0:T(8,128)S(1)}, s32[4,32,32]{2,1,0:T(8,128)}, u32[]{:S(2)}) copy-start(s32[4,32,32]{2,1,0:T(8,128)} %param.14) | copy-start | bytes 49156
  (54 other events, 250.9 us)

commit v2 on v1

--- a/solution.py
+++ b/solution.py
@@ -358,111 +358,6 @@
     qm=(lane==lab).astype(BF)
     km=jnp.where((lane!=lab)&(lane<4),-1e30,0.0).astype(BF)
     return qm,km
-
-def attn_fwd_kernel(q_ref,k_ref,v_ref,qm_ref,km_ref,o_ref,lse_ref,*,scale,qb):
-    p=pl.program_id(0)
-    cells=q_ref.shape[0]
-    nq=cells//qb
-    lane=lax.broadcasted_iota(jnp.int32,(1,128),1)
-    @pl.when(p==0)
-    def _():
-        lse_ref[...]=jnp.zeros_like(lse_ref)
-    for h in range(2):
-        mine=(lane//64)==h
-        k=jnp.where(mine,k_ref[...],km_ref[...])
-        def body(i,c):
-            rows=pl.ds(pl.multiple_of(i*qb,qb),qb)
-            q=jnp.where(mine,q_ref[rows,:]*jnp.asarray(scale,BF),qm_ref[rows,:])
-            s=lax.dot_general(q,k,NT,preferred_element_type=F32)
-            m=jnp.max(s,axis=1,keepdims=True)
-            e=jnp.exp(s-m)
-            l=jnp.sum(e,axis=1,keepdims=True)
-            a=(e*(1.0/l)).astype(BF)
-            o=lax.dot_general(a,v_ref[...],(((1,),(0,)),((),())),preferred_element_type=F32).astype(BF)
-            if h==0:
-                o_ref[rows,:]=o
-            else:
-                o_ref[rows,:]=jnp.where(mine,o,o_ref[rows,:])
-            lse_ref[rows,:]=jnp.where(lane==2*p+h,m+jnp.log(l),lse_ref[rows,:])
-            return c
-        lax.fori_loop(0,nq,body,0)
-
-def attn_fwd(projected,qm,km,features,qb=256):
-    cells=projected.shape[0]
-    pairs=features//128
-    blk=lambda off: pl.BlockSpec((cells,128),lambda p: (0,off+p))
-    full=pl.BlockSpec((cells,128),lambda p:(0,0))
-    return pl.pallas_call(
-        functools.partial(attn_fwd_kernel,scale=0.125,qb=qb),
-        grid=(pairs,),
-        in_specs=[blk(0),blk(pairs),blk(2*pairs),full,full],
-        out_specs=[blk(0),full],
-        out_shape=[jax.ShapeDtypeStruct((cells,features),BF),jax.ShapeDtypeStruct((cells,128),F32)],
-        compiler_params=pltpu.CompilerParams(dimension_semantics=("arbitrary",),vmem_limit_bytes=60<<20),
-        name="attn_fwd",
-    )(projected,projected,projected,qm,km)
-
-def attn_bwd_kernel(q_ref,k_ref,v_ref,do_ref,o_ref,qm_ref,km_ref,lse_ref,dq_ref,dk_ref,dv_ref,qs,dqt,*,scale,kb):
-    p=pl.program_id(0)
-    cells=q_ref.shape[0]
-    nk=cells//kb
-    lane=lax.broadcasted_iota(jnp.int32,(1,128),1)
-    sub=lax.broadcasted_iota(jnp.int32,(128,1),0)
-    prod=do_ref[...].astype(F32)*o_ref[...].astype(F32)
-    hi=prod.astype(BF); lo=(prod-hi.astype(F32)).astype(BF)
-    srow=lax.broadcasted_iota(jnp.int32,(8,128),0)
-    slane=lax.broadcasted_iota(jnp.int32,(8,128),1)
-    sel=(slane//64==srow).astype(BF)
-    delta=lax.dot_general(sel,hi,NT,preferred_element_type=F32)+lax.dot_general(sel,lo,NT,preferred_element_type=F32)
-    qs[...]=q_ref[...]*jnp.asarray(scale,BF)
-    for h in range(2):
-        mine=(lane//64)==h
-        q=jnp.where(mine,qs[...],qm_ref[...])
-        lse=lse_ref[pl.ds(2*p+h,1),:]
-        dl=delta[h:h+1,:]
-        dqt[...]=jnp.zeros_like(dqt)
-        def body(i,c):
-            rows=pl.ds(pl.multiple_of(i*kb,kb),kb)
-            kr=k_ref[rows,:]
-            k=jnp.where(mine,kr,km_ref[rows,:])
-            v=jnp.where(mine,v_ref[rows,:],jnp.zeros((),BF))
-            st=lax.dot_general(k,q,NT,preferred_element_type=F32)
-            pt=jnp.exp(st-lse)
-            dpt=lax.dot_general(v,do_ref[...],NT,preferred_element_type=F32)
-            ds=(pt*(dpt-dl)).astype(BF)
-            dv=lax.dot_general(pt.astype(BF),do_ref[...],(((1,),(0,)),((),())),preferred_element_type=F32).astype(BF)
-            dk=lax.dot_general(ds,qs[...],(((1,),(0,)),((),())),preferred_element_type=F32).astype(BF)
-            dqt[...]+=lax.dot_general(kr,ds,TN,preferred_element_type=F32)
-            if h==0:
-                dv_ref[rows,:]=dv
-                dk_ref[rows,:]=dk
-            else:
-                dv_ref[rows,:]=jnp.where(mine,dv,dv_ref[rows,:])
-                dk_ref[rows,:]=jnp.where(mine,dk,dk_ref[rows,:])
-            return c
-        lax.fori_loop(0,nk,body,0)
-        dq=(jnp.transpose(dqt[...])*scale).astype(BF)
-        if h==0:
-            dq_ref[...]=dq
-        else:
-            dq_ref[...]=jnp.where(mine,dq,dq_ref[...])
-
-def attn_bwd(projected,dout,out,qm,km,lse_t,features,kb=256):
-    cells=projected.shape[0]
-    pairs=features//128
-    blk=lambda off: pl.BlockSpec((cells,128),lambda p: (0,off+p))
-    full=pl.BlockSpec((cells,128),lambda p:(0,0))
-    o=jax.ShapeDtypeStruct((cells,features),BF)
-    return pl.pallas_call(
-        functools.partial(attn_bwd_kernel,scale=0.125,kb=kb),
-        grid=(pairs,),
-        in_specs=[blk(0),blk(pairs),blk(2*pairs),blk(0),blk(0),full,full,pl.BlockSpec((128,cells),lambda p:(0,0))],
-        out_specs=[blk(0),blk(0),blk(0)],
-        out_shape=[o,o,o],
-        scratch_shapes=[pltpu.VMEM((cells,128),BF),pltpu.VMEM((128,cells),F32)],
-        compiler_params=pltpu.CompilerParams(dimension_semantics=("arbitrary",),vmem_limit_bytes=60<<20),
-        name="attn_bwd",
-    )(projected,projected,projected,dout,out,qm,km,lse_t)
 
 MESH=pl.DeviceIdType.MESH
 NZ,NC,NR=4,2,4
@@ -689,28 +584,228 @@
 
 def sem_types(shapes):
     return [pltpu.SemaphoreType.DMA(s) for s in shapes]
+class GatherZ:
+    SEMS=[(NZ,),(NZ,),(1,)]
+    def __init__(self,shard,zp,sems):
+        self.shard,self.zp=shard,zp
+        self.s,self.r,self.lo=sems
+        self.z,self.core,self.rows=here()
+    def copy(self,dz,receive=False):
+        to=zmod(self.z+dz)
+        frm=zmod(self.z-dz)
+        return rcopy(self.shard,self.zp.at[frm if receive else self.z],self.s.at[dz],self.r.at[dz],dev(to,self.core,self.rows))
+    def local(self):
+        return pltpu.make_async_copy(self.shard,self.zp.at[self.z],self.lo.at[0])
+    def start(self):
+        for dz in range(1,NZ): self.copy(dz).start()
+        self.local().start()
+    def wait(self):
+        for dz in range(1,NZ): self.copy(dz,True).wait_recv()
+    def finish(self):
+        for dz in range(1,NZ): self.copy(dz).wait_send()
+        self.local().wait()
+
+
+class GatherXY:
+    SEMS=[(NZ,NR),(NZ,NR),(NZ,NR),(NZ,NR),(1,)]
+    def __init__(self,zp,full,sems):
+        self.zp,self.full=zp,full
+        self.sx,self.rx,self.sc,self.rc,self.lo=sems
+        self.z,self.core,self.rows=here()
+    def place(self,t):
+        return self.rows if t==0 else partner_xy(self.rows,t)
+    def xcopy(self,k,t,receive=False):
+        return rcopy(self.zp.at[k],self.full.at[k,self.core,self.place(t) if receive else self.rows],self.sx.at[k,t],self.rx.at[k,t],dev(self.z,self.core,self.place(t)))
+    def ccopy(self,k,t,receive=False):
+        src=self.zp.at[k] if t==0 else self.full.at[k,self.core,self.place(t)]
+        dst=self.full.at[k,1-self.core if receive else self.core,self.place(t)]
+        return rcopy(src,dst,self.sc.at[k,t],self.rc.at[k,t],dev(self.z,1-self.core,self.rows))
+    def local(self):
+        return pltpu.make_async_copy(self.zp,self.full.at[:,self.core,self.rows],self.lo.at[0])
+    def start(self,ks=range(NZ)):
+        for k in ks:
+            for t in range(1,NR): self.xcopy(k,t).start()
+            self.ccopy(k,0).start()
+    def start_local(self):
+        self.local().start()
+    def step(self,k):
+        for t in range(1,NR):
+            self.xcopy(k,t,True).wait_recv()
+            self.ccopy(k,t).start()
+    def arrive(self,k):
+        for t in range(NR): self.ccopy(k,t,True).wait_recv()
+    def finish(self):
+        for k in range(NZ):
+            for t in range(NR):
+                if t: self.xcopy(k,t).wait_send()
+                self.ccopy(k,t).wait_send()
+        self.local().wait()
+    def finish_remote(self):
+        for k in range(NZ):
+            for t in range(NR):
+                if t: self.xcopy(k,t).wait_send()
+                self.ccopy(k,t).wait_send()
+
+
+class ScatterZ:
+    SEMS=[(NZ,),(NZ,)]
+    @staticmethod
+    def scratch(r,c,dt):
+        return [pltpu.VMEM((NZ,r,c),dt)]
+    def __init__(self,zout,out,bufs,sems):
+        self.zout,self.out=zout,out
+        self.zin,=bufs
+        self.s,self.r=sems
+        self.z,self.core,self.rows=here()
+    def copy(self,dz):
+        to=zmod(self.z+dz)
+        return rcopy(self.zout.at[to],self.zin.at[dz],self.s.at[dz],self.r.at[dz],dev(to,self.core,self.rows))
+    def start(self):
+        for dz in range(1,NZ): self.copy(dz).start()
+    def step(self):
+        for dz in range(1,NZ): self.copy(dz).wait_recv()
+        v=self.zout[self.z].astype(F32)
+        for dz in range(1,NZ): v=v+self.zin[dz].astype(F32)
+        self.out[...]=v
+    def finish(self):
+        for dz in range(1,NZ): self.copy(dz).wait_send()
+
+
+class Events:
+    def __init__(self): self.at={}
+    def add(self,slot,fn): self.at.setdefault(slot,[]).append(fn)
+    def run(self,outer,inner,width):
+        for slot,fns in self.at.items():
+            if slot%width==inner:
+                @pl.when(outer==slot//width)
+                def _(fns=fns):
+                    for fn in fns: fn()
+NN=(((1,),(0,)),((),()))
+C0=0.7978845608028654
+C1=0.044715
+
+
+def dotf(a,b,dims=NN):
+    return lax.dot_general(a,b,dims,preferred_element_type=F32)
+
+
+def loop(n,fn,unroll=1):
+    def body(i,c):
+        fn(i); return c
+    lax.fori_loop(0,n,body,0,unroll=unroll)
+
+
+def rows_of(i,n):
+    return pl.ds(pl.multiple_of(i*n,n),n)
+
+
+def normal_rows(v):
+    d=1.0/v.shape[1]
+    c=v-jnp.sum(v,axis=1,keepdims=True)*d
+    inv=lax.rsqrt(jnp.sum(c*c,axis=1,keepdims=True)*d+EPSILON)
+    return c*inv,inv
+
+
+def normal_back_rows(g,n,inv):
+    d=1.0/g.shape[1]
+    return inv*(g-jnp.sum(g,axis=1,keepdims=True)*d-n*(jnp.sum(g*n,axis=1,keepdims=True)*d))
+
+
+def fold8(v):
+    s=v[0:8]
+    for k in range(1,v.shape[0]//8): s=s+v[8*k:8*k+8]
+    return s
+
+
+def conv_loops(side,lanes_n,width,forward,finish):
+    pass
+
+
+def shifts(f,ml,mr):
+    n=f.shape[0]
+    return pltpu.roll(f,1,0)*ml, pltpu.roll(f,n-1,0)*mr
+
+
+def conv_rows(src,dst_fn,taps,ml_ref,mr_ref,rl_ref,lane,side,cols):
+    sl=pl.ds(lane*128,128)
+    k=[taps[q:q+1,lane*128:(lane+1)*128] for q in range(9)]
+    zero=jnp.zeros((cols,128),F32)
+    def body(i,c):
+        hm,part=c
+        f=src[rows_of(i,cols),lane*128:(lane+1)*128]
+        fm,fp=shifts(f,ml_ref[rows_of(i,cols),:],mr_ref[rows_of(i,cols),:])
+        h=[k[3*a]*fm+k[3*a+1]*f+k[3*a+2]*fp for a in range(3)]
+        done=part+rl_ref[i]*h[2]
+        @pl.when(i>0)
+        def _(): dst_fn(i-1,done)
+        return h[0],h[1]+rl_ref[i]*hm
+    hm,part=lax.fori_loop(0,side,body,(zero,zero),unroll=4)
+    dst_fn(side-1,part)
+
+
+def back_rows(g_ref,f_ref,dst_fn,taps,ml_ref,mr_ref,rl_ref,lane,side,cols):
+    ls=slice(lane*128,(lane+1)*128)
+    k=[taps[q:q+1,ls] for q in range(9)]
+    zero=jnp.zeros((cols,128),F32)
+    z8=jnp.zeros((8,128),F32)
+    def body(i,c):
+        hp,part,fprev,acc=c
+        g=g_ref[rows_of(i,cols),ls]
+        gm,gp=shifts(g,ml_ref[rows_of(i,cols),:],mr_ref[rows_of(i,cols),:])
+        gs=(gp,g,gm)
+        q=[k[3*a]*gp+k[3*a+1]*g+k[3*a+2]*gm for a in range(3)]
+        done=part+rl_ref[i]*q[0]
+        @pl.when(i>0)
+        def _(): dst_fn(i-1,done)
+        f=f_ref[rows_of(i,cols),ls]
+        nxt=f_ref[pl.ds(pl.multiple_of(jnp.minimum(i+1,side-1)*cols,cols),cols),ls]
+        fs=(fprev*rl_ref[i],f,nxt*rl_ref[i+1])
+        acc=tuple(acc[3*a+b]+fold8(fs[a]*gs[b]) for a in range(3) for b in range(3))
+        return q[2],q[1]+rl_ref[i]*hp,f,acc
+    hp,part,_,acc=lax.fori_loop(0,side,body,(zero,zero,zero,(z8,)*9),unroll=4)
+    dst_fn(side-1,part)
+    return acc
+
+
+def link_masks(labels):
+    side,cols=labels.shape
+    left=jnp.pad(labels[:,1:]==labels[:,:-1],((0,0),(1,0)))
+    right=jnp.pad(labels[:,1:]==labels[:,:-1],((0,0),(0,1)))
+    wide=lambda m: jnp.broadcast_to(m.reshape(side*cols,1).astype(F32),(side*cols,128))
+    top=labels[:,0]//2
+    rl=jnp.pad((top[1:]==top[:-1]).astype(F32),(1,1))
+    return wide(left),wide(right),rl
 HBM=pl.BlockSpec(memory_space=pl.ANY)
 VM=pl.BlockSpec(memory_space=pltpu.VMEM)
+SM=pl.BlockSpec(memory_space=pltpu.SMEM)
 NDEV=NZ*NC*NR
-
-
-def enter_kernel(n_w,*refs):
+S_=jax.ShapeDtypeStruct
+
+
+def taker(it):
+    return lambda cls:[next(it) for _ in cls.SEMS]
+
+
+def enter_kernel(n_z,*refs):
     it=iter(refs)
-    tok,cot,cond,ada,bias=[next(it) for _ in range(5)]
-    shards=[next(it) for _ in range(n_w)]
-    tok_o,cot_o,cond_o,mod_o=[next(it) for _ in range(4)]
-    fulls=[next(it) for _ in range(n_w)]
-    condv,part,modin=[next(it) for _ in range(3)]
-    take=lambda cls:[next(it) for _ in cls.SEMS]
+    tok,cond,ada,bias,qkv,taps=[next(it) for _ in range(6)]
+    shards=[next(it) for _ in range(n_z)]
+    tok_o,cond_o,mod_o,qkv_o,taps_o=[next(it) for _ in range(5)]
+    zps=[next(it) for _ in range(n_z)]
+    condv,part=[next(it) for _ in range(2)]
+    mbufs=[next(it) for _ in range(5)]
+    take=taker(it)
     barrier_all()
     c_all=AllToAll(cond,condv,take(AllToAll),one=True)
     swap_t=Swap(tok,tok_o,take(Swap))
-    swap_c=Swap(cot,cot_o,take(Swap))
-    m_all=AllToAll(part,modin,take(AllToAll))
-    gathers=[Gather(s,f,take(Gather)) for s,f in zip(shards,fulls)]
+    m_all=Scatter(part,mod_o,mbufs,take(Scatter))
+    g_taps=Gather(taps,taps_o,take(Gather))
+    g_qkv=Gather(qkv,qkv_o,take(Gather))
+    gz=[GatherZ(s,z,take(GatherZ)) for s,z in zip(shards,zps)]
     c_all.start()
     swap_t.start()
-    gathers[0].start()
+    g_taps.start()
+    g_qkv.start()
     c_all.wait()
     me=c_all.me
     feats=ada.shape[0]
@@ -724,62 +819,219 @@
         pr=jnp.dot(mine,ada[:,c*chunk:(c+1)*chunk],preferred_element_type=F32)
         for l in range(chunk//128):
             i=c*(chunk//128)+l
-            part[:,i,:]=pr[:,l*128:(l+1)*128]+bias[i:i+1,:]
+            part[:,:,:,i,:]=(pr[:,l*128:(l+1)*128]+bias[i:i+1,:]).reshape(NZ,NC,NR,128)
     cond_o[...]=low
     m_all.start()
-    gathers[0].run_z()
-    for g in gathers[1:]: g.start()
-    m_all.wait()
-    s=modin[0]
-    def add(i,s): return s+modin[i]
-    mod_o[...]=lax.fori_loop(1,NDEV,add,s)
+    m_all.cstep()
+    g_taps.run_z(); g_qkv.run_z()
+    m_all.xstep()
+    for g in gz: g.start()
+    m_all.zstep()
     swap_t.wait()
-    gathers[0].run_x()
-    for g in gathers[1:]:
-        g.run_z()
-    swap_c.start()
-    for g in gathers[1:]:
-        g.run_x()
-    swap_c.wait()
-    for g in gathers: g.finish()
-    swap_t.finish(); swap_c.finish(); c_all.finish(); m_all.finish()
-
-
-def enter(tok,cot,cond_row,ada,bias_rows,shards):
-    n_w=len(shards)
-    scr=[pltpu.VMEM((NDEV,)+cond_row.shape,cond_row.dtype),pltpu.VMEM((NDEV,)+bias_rows.shape,F32),pltpu.VMEM((NDEV,)+bias_rows.shape,F32)]
-    sems=sem_types(AllToAll.SEMS)+sem_types(Swap.SEMS)*2+sem_types(AllToAll.SEMS)+sem_types(Gather.SEMS)*n_w
-    outs=[jax.ShapeDtypeStruct(tok.shape,tok.dtype),jax.ShapeDtypeStruct(cot.shape,cot.dtype),
-          jax.ShapeDtypeStruct((NDEV,cond_row.shape[1]),BF),jax.ShapeDtypeStruct(bias_rows.shape,F32)]
-    outs+=[jax.ShapeDtypeStruct((NZ,NC,NR)+s.shape,s.dtype) for s in shards]
+    g_taps.run_x(); g_qkv.run_x()
+    for g in gz: g.wait()
+    for g in [g_taps,g_qkv,swap_t,c_all,m_all]+gz: g.finish()
+
+
+def enter(tok,cond_row,ada,bias_rows,qkv,taps,shards):
+    n=len(shards)
+    scr=[pltpu.VMEM((NDEV,)+cond_row.shape,cond_row.dtype),pltpu.VMEM((NZ,NC,NR)+bias_rows.shape,F32)]+Scatter.scratch(bias_rows.shape[0],128,F32)
+    sems=sem_types(AllToAll.SEMS)+sem_types(Swap.SEMS)+sem_types(Scatter.SEMS)+sem_types(Gather.SEMS)*2+sem_types(GatherZ.SEMS)*n
+    outs=[S_(tok.shape,tok.dtype),S_((NDEV,cond_row.shape[1]),BF),S_(bias_rows.shape,F32),
+          S_((NZ,NC,NR)+qkv.shape,qkv.dtype),S_((NZ,NC,NR)+taps.shape,taps.dtype)]
+    outs+=[S_((NZ,)+s.shape,s.dtype) for s in shards]
     return pl.pallas_call(
-        functools.partial(enter_kernel,n_w),
-        in_specs=[HBM,HBM,HBM,VM,VM]+[HBM]*n_w,
-        out_specs=[HBM,HBM,VM,VM]+[HBM]*n_w,
+        functools.partial(enter_kernel,n),
+        in_specs=[HBM,HBM,VM,VM,HBM,HBM]+[HBM]*n,
+        out_specs=[HBM,VM,VM,HBM,HBM]+[HBM]*n,
         out_shape=outs,
         scratch_shapes=scr+sems,
         compiler_params=pltpu.CompilerParams(collective_id=0,has_side_effects=True,vmem_limit_bytes=48<<20),
         name="enter",
-    )(tok,cot,cond_row,ada,bias_rows,*shards)
-
-
-def leave_kernel(n_g,refs_spec,*refs):
+    )(tok,cond_row,ada,bias_rows,qkv,taps,*shards)
+
+
+def forward_kernel(n_w,qb,*refs):
     it=iter(refs)
-    lay,tg,gm,low,ada=[next(it) for _ in range(5)]
+    mix,qkv,qm,km,cot,late=[next(it) for _ in range(6)]
+    zps=[next(it) for _ in range(n_w)]
+    proj,att,lse_t,cot_o,late_o=[next(it) for _ in range(5)]
+    fulls=[next(it) for _ in range(n_w)]
+    lse=next(it)
+    take=taker(it)
+    barrier_all()
+    swap_c=Swap(cot,cot_o,take(Swap))
+    gs=[GatherXY(a,b,take(GatherXY)) for a,b in zip(zps,fulls)]
+    gl=GatherZ(late,late_o,take(GatherZ))
+    gl.start()
+    gs[0].start(); swap_c.start(); gs[1].start()
+    for g in gs: g.start_local()
+    ev=Events()
+    for k in range(NZ):
+        ev.add(1,lambda k=k: gs[0].step(k))
+        ev.add(8+k,lambda k=k: gs[1].step(k))
+    cells,feat=att.shape
+    CH=256
+    def pr(i):
+        proj[rows_of(i,CH),:]=dotf(mix[rows_of(i,CH),:],qkv[...]).astype(BF)
+    loop(cells//CH,pr)
+    pairs=feat//128
+    lane=lax.broadcasted_iota(jnp.int32,(1,128),1)
+    lse[...]=jnp.zeros_like(lse)
+    def pair(p):
+        cq=pl.ds(pl.multiple_of(p*128,128),128)
+        ck=pl.ds(pl.multiple_of(feat+p*128,128),128)
+        cv=pl.ds(pl.multiple_of(2*feat+p*128,128),128)
+        for h in range(2):
+            ev.run(p,h,2)
+            mine=(lane//64)==h
+            k=jnp.where(mine,proj[:,ck],km[...])
+            def body(i):
+                r=rows_of(i,qb)
+                q=jnp.where(mine,proj[r,cq]*jnp.asarray(0.125,BF),qm[r,:])
+                s=dotf(q,k,NT)
+                m=jnp.max(s,axis=1,keepdims=True)
+                e=jnp.exp(s-m)
+                l=jnp.sum(e,axis=1,keepdims=True)
+                a=(e*(1.0/l)).astype(BF)
+                o=dotf(a,proj[:,cv]).astype(BF)
+                if h==0:
+                    att[r,cq]=o
+                else:
+                    att[r,cq]=jnp.where(mine,o,att[r,cq])
+                lse[r,:]=jnp.where(lane==2*p+h,m+jnp.log(l),lse[r,:])
+            loop(cells//qb,body)
+    loop(pairs,pair)
+    lse_t[...]=jnp.transpose(lse[...])
+    for g in gs:
+        for k in range(NZ): g.arrive(k)
+    swap_c.wait()
+    gl.wait()
+    for g in gs+[swap_c,gl]: g.finish()
+
+
+def forward(mix,qkv,qm,km,cot,late,zps):
+    n=len(zps)
+    cells,feat=mix.shape
+    outs=[S_((cells,3*feat),BF),S_((cells,feat),BF),S_((128,cells),F32),S_(cot.shape,cot.dtype),S_((NZ,)+late.shape,late.dtype)]
+    outs+=[S_((NZ,NC,NR)+z.shape[1:],z.dtype) for z in zps]
+    return pl.pallas_call(
+        functools.partial(forward_kernel,n,256),
+        in_specs=[VM,VM,VM,VM,HBM,HBM]+[HBM]*n,
+        out_specs=[VM,VM,VM,HBM,HBM]+[HBM]*n,
+        out_shape=outs,
+        scratch_shapes=[pltpu.VMEM((cells,128),F32)]+sem_types(Swap.SEMS)+sem_types(GatherXY.SEMS)*n+sem_types(GatherZ.SEMS),
+        compiler_params=pltpu.CompilerParams(collective_id=1,has_side_effects=True,vmem_limit_bytes=60<<20),
+        name="attn_fwd",
+    )(mix,qkv,qm,km,cot,late,*zps)
+
+
+def backward_kernel(n_g,kb,*refs):
+    it=iter(refs)
+    proj,do,o,qm,km,lse_t,lay,gout=[next(it) for _ in range(8)]
     parts=[next(it) for _ in range(n_g)]
-    lay_o,tg_o,ctx_o,adag_o,gm_o=[next(it) for _ in range(5)]
+    gp,lay_o,gout_o=[next(it) for _ in range(3)]
+    gouts=[next(it) for _ in range(n_g)]
+    qs,dqt=[next(it) for _ in range(2)]
+    obufs=[next(it) for _ in range(5)]
+    bufs=[[next(it) for _ in range(1)] for _ in range(n_g)]
+    take=taker(it)
+    barrier_all()
+    sl=Swap(lay,lay_o,take(Swap))
+    so=Scatter(gout,gout_o,obufs,take(Scatter))
+    sc=[ScatterZ(p,g,b,take(ScatterZ)) for p,g,b in zip(parts,gouts,bufs)]
+    ev=Events()
+    so.start()
+    for s in sc: s.start()
+    sl.start()
+    ev.add(1,so.cstep)
+    ev.add(6,so.xstep)
+    for s in sc: ev.add(8,s.step)
+    ev.add(11,so.zstep)
+    cells,feat=do.shape
+    pairs=feat//128
+    lane=lax.broadcasted_iota(jnp.int32,(1,128),1)
+    srow=lax.broadcasted_iota(jnp.int32,(8,128),0)
+    slane=lax.broadcasted_iota(jnp.int32,(8,128),1)
+    sel=(slane//64==srow).astype(BF)
+    def pair(p):
+        cq=pl.ds(pl.multiple_of(p*128,128),128)
+        ck=pl.ds(pl.multiple_of(feat+p*128,128),128)
+        cv=pl.ds(pl.multiple_of(2*feat+p*128,128),128)
+        prod=do[:,cq].astype(F32)*o[:,cq].astype(F32)
+        hi=prod.astype(BF); lo=(prod-hi.astype(F32)).astype(BF)
+        delta=dotf(sel,hi,NT)+dotf(sel,lo,NT)
+        qs[...]=proj[:,cq]*jnp.asarray(0.125,BF)
+        for h in range(2):
+            ev.run(p,h,2)
+            mine=(lane//64)==h
+            q=jnp.where(mine,qs[...],qm[...])
+            ls=lse_t[pl.ds(2*p+h,1),:]
+            dl=delta[h:h+1,:]
+            dqt[...]=jnp.zeros_like(dqt)
+            def body(i):
+                r=rows_of(i,kb)
+                kr=proj[r,ck]
+                k=jnp.where(mine,kr,km[r,:])
+                v=jnp.where(mine,proj[r,cv],jnp.zeros((),BF))
+                st=dotf(k,q,NT)
+                pt=jnp.exp(st-ls)
+                dpt=dotf(v,do[:,cq],NT)
+                ds=(pt*(dpt-dl)).astype(BF)
+                dv=dotf(pt.astype(BF),do[:,cq]).astype(BF)
+                dk=dotf(ds,qs[...]).astype(BF)
+                dqt[...]+=dotf(kr,ds,TN)
+                if h==0:
+                    gp[r,cv]=dv
+                    gp[r,ck]=dk
+                else:
+                    gp[r,cv]=jnp.where(mine,dv,gp[r,cv])
+                    gp[r,ck]=jnp.where(mine,dk,gp[r,ck])
+            loop(cells//kb,body)
+            dq=(jnp.transpose(dqt[...])*0.125).astype(BF)
+            if h==0:
+                gp[:,cq]=dq
+            else:
+                gp[:,cq]=jnp.where(mine,dq,gp[:,cq])
+    loop(pairs,pair)
+    sl.wait()
+    for s in sc+[sl,so]: s.finish()
+
+
+def backward(proj,do,o,qm,km,lse_t,lay,gout,parts):
+    n=len(parts)
+    cells,feat=do.shape
+    outs=[S_((cells,3*feat),BF),S_(lay.shape,lay.dtype),S_(gout.shape[3:],F32)]+[S_(p.shape[1:],F32) for p in parts]
+    scr=[pltpu.VMEM((cells,128),BF),pltpu.VMEM((128,cells),F32)]+Scatter.scratch(gout.shape[3],gout.shape[4],gout.dtype)
+    for p in parts: scr+=ScatterZ.scratch(p.shape[1],p.shape[2],p.dtype)
+    return pl.pallas_call(
+        functools.partial(backward_kernel,n,256),
+        in_specs=[VM,VM,VM,VM,VM,VM,HBM,HBM]+[VM]*n,
+        out_specs=[VM,HBM,VM]+[VM]*n,
+        out_shape=outs,
+        scratch_shapes=scr+sem_types(Swap.SEMS)+sem_types(Scatter.SEMS)+sem_types(ScatterZ.SEMS)*n,
+        compiler_params=pltpu.CompilerParams(collective_id=2,has_side_effects=True,vmem_limit_bytes=62<<20),
+        name="attn_bwd",
+    )(proj,do,o,qm,km,lse_t,lay,gout,*parts)
+
+
+def leave_kernel(n_g,*refs):
+    it=iter(refs)
+    tg,gm,low,ada=[next(it) for _ in range(4)]
+    parts=[next(it) for _ in range(n_g)]
+    tg_o,ctx_o,adag_o,gm_o=[next(it) for _ in range(4)]
     gouts=[next(it) for _ in range(n_g)]
     gmv,ctxs,ctxv=[next(it) for _ in range(3)]
     bufs=[[next(it) for _ in range(5)] for _ in range(n_g)]
-    take=lambda cls:[next(it) for _ in cls.SEMS]
+    take=taker(it)
     barrier_all()
     g_all=AllToAll(gm,gmv,take(AllToAll),one=True)
     x_all=AllToAll(ctxs,ctxv,take(AllToAll))
-    sl=Swap(lay,lay_o,take(Swap)); st=Swap(tg,tg_o,take(Swap))
+    st=Swap(tg,tg_o,take(Swap))
     sc=[Scatter(p,o,b,take(Scatter)) for p,o,b in zip(parts,gouts,bufs)]
     g_all.start()
     for s in sc: s.start()
-    st.start(); sl.start()
+    st.start()
     g_all.wait()
     me=g_all.me
     feats=ada.shape[0]
@@ -801,31 +1053,282 @@
     ctx_o[...]=ctxv[...]
     for s in sc: s.xstep()
     for s in sc: s.zstep()
-    st.wait(); sl.wait()
+    st.wait()
     for s in sc: s.finish()
-    st.finish(); sl.finish(); g_all.finish(); x_all.finish()
-
-
-def leave(lay,tg,gm,low,ada,parts):
+    st.finish(); g_all.finish(); x_all.finish()
+
+
+def leave(tg,gm,low,ada,parts):
     n_g=len(parts)
-    cols=ada.shape[1]
     scr=[pltpu.VMEM((NDEV,)+gm.shape,gm.dtype),pltpu.VMEM((NDEV,8,128),F32),pltpu.VMEM((NDEV,8,128),F32)]
     for p in parts: scr+=Scatter.scratch(p.shape[3],p.shape[4],p.dtype)
-    sems=sem_types(AllToAll.SEMS)*2+sem_types(Swap.SEMS)*2+sem_types(Scatter.SEMS)*n_g
-    outs=[jax.ShapeDtypeStruct(lay.shape,lay.dtype),jax.ShapeDtypeStruct(tg.shape,tg.dtype),
-          jax.ShapeDtypeStruct((NDEV,8,128),F32),jax.ShapeDtypeStruct(ada.shape,F32),jax.ShapeDtypeStruct(gm.shape,F32)]
-    outs+=[jax.ShapeDtypeStruct(p.shape[3:],F32) for p in parts]
+    sems=sem_types(AllToAll.SEMS)*2+sem_types(Swap.SEMS)+sem_types(Scatter.SEMS)*n_g
+    outs=[S_(tg.shape,tg.dtype),S_((NDEV,8,128),F32),S_(ada.shape,F32),S_(gm.shape,F32)]
+    outs+=[S_(p.shape[3:],F32) for p in parts]
     return pl.pallas_call(
-        functools.partial(leave_kernel,n_g,None),
-        in_specs=[HBM,HBM,HBM,VM,VM]+[HBM]*n_g,
-        out_specs=[HBM,HBM,VM,VM,VM]+[VM]*n_g,
+        functools.partial(leave_kernel,n_g),
+        in_specs=[HBM,HBM,VM,VM]+[HBM]*n_g,
+        out_specs=[HBM,VM,VM,VM]+[VM]*n_g,
         out_shape=outs,
         scratch_shapes=scr+sems,
-        compiler_params=pltpu.CompilerParams(collective_id=1,has_side_effects=True,vmem_limit_bytes=60<<20),
+        compiler_params=pltpu.CompilerParams(collective_id=3,has_side_effects=True,vmem_limit_bytes=60<<20),
         name="leave",
-    )(lay,tg,gm,low,ada,*parts)
-
-
+    )(tg,gm,low,ada,*parts)
+def greet(targets):
+    bar=pltpu.get_barrier_semaphore()
+    for d in targets:
+        pl.semaphore_signal(bar,inc=1,device_id=d,device_id_type=MESH)
+    pl.semaphore_wait(bar,len(targets))
+
+
+def near():
+    z,core,rows=here()
+    return [dev(z,1-core,rows)]+[dev(z,core,partner_xy(rows,t)) for t in range(1,NR)]
+
+
+class PipeScatter:
+    SEMS=[(2,),(2,),(2,NR),(2,NR)]
+    @staticmethod
+    def scratch(r,c):
+        return [pltpu.VMEM((2,NZ,NC,NR,r,c),BF),pltpu.VMEM((2,NZ,NR,r,c),BF),pltpu.VMEM((2,NZ,NR,r,c),BF),pltpu.VMEM((2,NR,NZ,r,c),BF)]
+    def __init__(self,bufs,sems):
+        self.part,self.sib,self.own,self.xin=bufs
+        self.sc,self.rc,self.sx,self.rx=sems
+        self.z,self.core,self.rows=here()
+    def ccopy(self,s):
+        return rcopy(self.part.at[s,:,1-self.core],self.sib.at[s],self.sc.at[s],self.rc.at[s],dev(self.z,1-self.core,self.rows))
+    def xcopy(self,s,t):
+        to=partner_xy(self.rows,t)
+        return rcopy(self.own.at[s,:,to],self.xin.at[s,t],self.sx.at[s,t],self.rx.at[s,t],dev(self.z,self.core,to))
+    def send_core(self,s):
+        self.ccopy(s).start()
+    def send_square(self,s):
+        self.ccopy(s).wait()
+        def body(i):
+            a,b=i//NR,lax.rem(i,NR)
+            self.own[s,a,b]=(self.part[s,a,self.core,b].astype(F32)+self.sib[s,a,b].astype(F32)).astype(BF)
+        loop(NZ*NR,body)
+        for t in range(1,NR): self.xcopy(s,t).start()
+    def collect(self,s,put):
+        for t in range(1,NR): self.xcopy(s,t).wait()
+        def body(a):
+            v=self.own[s,a,self.rows].astype(F32)
+            for t in range(1,NR): v=v+self.xin[s,t,a].astype(F32)
+            put(a,v.astype(BF))
+        loop(NZ,body)
+
+
+class RowScatter:
+    SEMS=[(2,),(2,),(2,NR),(2,NR)]
+    @staticmethod
+    def scratch(r,c):
+        return [pltpu.VMEM((2,NR,r,c),BF),pltpu.VMEM((2,NR,r,c),BF),pltpu.VMEM((2,NR,r,c),BF)]
+    def __init__(self,part,zout,bufs,sems):
+        self.part,self.zout=part,zout
+        self.sib,self.own,self.xin=bufs
+        self.sc,self.rc,self.sx,self.rx=sems
+        self.z,self.core,self.rows=here()
+    def ccopy(self,k):
+        s=k%2
+        return rcopy(self.part.at[k,1-self.core],self.sib.at[s],self.sc.at[s],self.rc.at[s],dev(self.z,1-self.core,self.rows))
+    def xcopy(self,k,t):
+        s=k%2
+        to=partner_xy(self.rows,t)
+        return rcopy(self.own.at[s,to],self.xin.at[s,t],self.sx.at[s,t],self.rx.at[s,t],dev(self.z,self.core,to))
+    def send_core(self,k):
+        self.ccopy(k).start()
+    def send_square(self,k):
+        self.ccopy(k).wait()
+        s=k%2
+        def body(b):
+            self.own[s,b]=(self.part[k,self.core,b].astype(F32)+self.sib[s,b].astype(F32)).astype(BF)
+        loop(NR,body)
+        for t in range(1,NR): self.xcopy(k,t).start()
+    def collect(self,k):
+        s=k%2
+        for t in range(1,NR): self.xcopy(k,t).wait()
+        v=self.own[s,self.rows].astype(F32)
+        for t in range(1,NR): v=v+self.xin[s,t].astype(F32)
+        self.zout[k]=v.astype(BF)
+
+
+def ffn_kernel_body(*refs,side,cols):
+    it=iter(refs)
+    nx=lambda n:[next(it) for _ in range(n)]
+    x_ref,att_ref,cot_ref,mod_ref,outw_ref,up_ref,zpd,tap_ref,ml_ref,mr_ref,rl_ref=nx(11)
+    lay_ref,gmid_ref,gatt_ref,gout_ref,zup,zdown,gtap_ref,sums_ref=nx(8)
+    m2,m2t,gffn,branch,middle,fb,gm2,F,G,glow,gub,dfull,gd=nx(13)
+    ubufs=nx(4); dbufs=nx(3)
+    take=taker(it)
+    ga=GatherXY(zpd,dfull,take(GatherXY))
+    us=PipeScatter(ubufs,take(PipeScatter))
+    ds=RowScatter(gd,zdown,dbufs,take(RowScatter))
+    t=pl.program_id(0)
+    cells,feat=x_ref.shape
+    T=up_ref.shape[1]
+    hidden=NDEV*zpd.shape[1]
+    steps=hidden//T; last=steps-1
+    block=hidden//NZ
+    CH=256; EC=32
+    shift2=mod_ref[3:4,:]; scale2=mod_ref[4:5,:]; gate2=mod_ref[5:6,:]; gate1=mod_ref[2:3,:]
+    slot=lax.rem(t,2); other=lax.rem(t+1,2)
+    ready={}
+    for k in range(NZ): ready[k]=-(-((k+1)*block)//T)-1
+    need={}
+    for k in range(NZ): need[k]=(k*block)//T
+    def put_up(tile):
+        def put(a,v): zup[a,:,pl.ds(pl.multiple_of(tile*T,128),T)]=v
+        return put
+
+    @pl.when(t==0)
+    def _():
+        greet(near())
+        ga.start(); ga.start_local()
+        def a(i):
+            branch[rows_of(i,CH),:]=dotf(att_ref[rows_of(i,CH),:],outw_ref[...])
+        loop(cells//CH,a)
+        def b(i):
+            r=rows_of(i,EC)
+            mid=x_ref[r,:].astype(F32)+gate1*branch[r,:]
+            middle[r,:]=mid
+            n,_=normal_rows(mid)
+            m2[r,:]=(n*(1.0+scale2)+shift2).astype(BF)
+            gffn[r,:]=(gate2*cot_ref[r,:].astype(F32)).astype(BF)
+        loop(cells//EC,b)
+        ga.step(0)
+        def c(i):
+            r=rows_of(i,CH)
+            m2t[:,pl.ds(pl.multiple_of(i*CH,CH),CH)]=jnp.transpose(m2[r,:])
+            fb[r,:]=jnp.zeros((CH,feat),F32)
+            gm2[r,:]=jnp.zeros((CH,feat),F32)
+        loop(cells//CH,c)
+        ga.local().wait()
+    for k in range(NZ):
+        @pl.when(t==need[k])
+        def _(k=k):
+            if k: ga.step(k)
+            ga.arrive(k)
+    @pl.when(t>=2)
+    def _():
+        us.collect(slot,put_up(t-2))
+    for k in range(NZ):
+        if ready[k]+2<=last:
+            @pl.when(t==ready[k]+2)
+            def _(k=k): ds.collect(k)
+
+    dw=dfull.reshape(hidden,feat)
+    gdw=gd.reshape(hidden,feat)
+    tr=pl.ds(pl.multiple_of(t*T,T),T)
+    def first(i):
+        r=rows_of(i,CH)
+        F[r,:]=dotf(m2[r,:],up_ref[...]).astype(BF).astype(F32)
+        G[r,:]=dotf(gffn[r,:],dw[tr,:],NT)
+    loop(cells//CH,first)
+
+    taps=tap_ref[...].astype(F32)
+    for lane in range(T//128):
+        ls=slice(lane*128,(lane+1)*128)
+        def put(i,u):
+            r=rows_of(i,cols)
+            u2=u*u
+            th=jnp.tanh(C0*(u+C1*(u2*u)))
+            half=0.5*(1.0+th)
+            glow[r,ls]=(u*half).astype(BF)
+            d=half+(0.5*u)*(1.0-th*th)*(C0*(1.0+(3.0*C1)*u2))
+            G[r,ls]=(G[r,ls]*d).astype(BF).astype(F32)
+        conv_rows(F,put,taps,ml_ref,mr_ref,rl_ref,lane,side,cols)
+    @pl.when(t>=1)
+    def _():
+        us.send_square(other)
+    for k in range(NZ):
+        if ready[k]+1<=last:
+            @pl.when(t==ready[k]+1)
+            def _(k=k): ds.send_square(k)
+    for lane in range(T//128):
+        ls=slice(lane*128,(lane+1)*128)
+        def put2(i,u):
+            gub[rows_of(i,cols),ls]=u.astype(BF)
+        acc=back_rows(G,F,put2,taps,ml_ref,mr_ref,rl_ref,lane,side,cols)
+        for q in range(9):
+            gtap_ref[q:q+1,ls]=jnp.sum(acc[q],axis=0,keepdims=True)
+    gtap_ref[9:16,:]=jnp.zeros((7,T),F32)
+
+    r_=feat//NDEV
+    def third(i):
+        n=NC*NR*r_
+        us.part[slot,i]=dotf(m2t[rows_of(i,n),:],gub[...]).astype(BF).reshape(NC,NR,r_,T)
+    loop(NZ,third)
+    us.send_core(slot)
+    for i in range(T//256):
+        gdw[pl.ds(pl.multiple_of(t*T+i*256,256),256),:]=dotf(glow[:,i*256:(i+1)*256],gffn[...],TN).astype(BF)
+    for k in range(NZ):
+        @pl.when(t==ready[k])
+        def _(k=k): ds.send_core(k)
+    def second(i):
+        r=rows_of(i,CH)
+        fb[r,:]+=dotf(glow[r,:],dw[tr,:])
+        gm2[r,:]+=dotf(gub[r,:],up_ref[...],NT)
+    loop(cells//CH,second)
+
+    @pl.when(t==last)
+    def _():
+        us.collect(other,put_up(last-1))
+        late=[k for k in range(NZ) if ready[k]+1>last]
+        mid_=[k for k in range(NZ) if ready[k]+1==last]
+        for k in mid_: ds.collect(k)
+        us.send_square(slot)
+        for k in late: ds.send_square(k)
+        z=jnp.zeros((8,feat),F32)
+        def body(i,c):
+            sg2,ss2,sc2,sg1=c
+            r=rows_of(i,EC)
+            inc=cot_ref[r,:].astype(F32)
+            mid=middle[r,:]
+            n,inv=normal_rows(mid)
+            lay_ref[r,:]=(mid+gate2*fb[r,:]).astype(BF)
+            gm=gm2[r,:]
+            gmid=inc+normal_back_rows(gm*(1.0+scale2),n,inv)
+            gmid_ref[r,:]=gmid
+            gffn[r,:]=(gate1*gmid).astype(BF)
+            return (sg2+fold8(inc*fb[r,:]),ss2+fold8(gm),sc2+fold8(gm*n),sg1+fold8(gmid*branch[r,:]))
+        res=lax.fori_loop(0,cells//EC,body,(z,z,z,z))
+        for q in range(4):
+            sums_ref[q:q+1,:]=jnp.sum(res[q],axis=0,keepdims=True)
+        sums_ref[4:8,:]=jnp.zeros((4,feat),F32)
+        def b(i):
+            r=rows_of(i,CH)
+            gatt_ref[r,:]=dotf(gffn[r,:],outw_ref[...],NT).astype(BF)
+        loop(cells//CH,b)
+        for i in range(feat//256):
+            gout_ref[i*256:(i+1)*256,:]=dotf(att_ref[:,i*256:(i+1)*256],gffn[...],TN).astype(BF)
+        us.collect(slot,put_up(last))
+        for k in late: ds.collect(k)
+        ga.finish_remote()
+
+
+def ffn(x,att,cot,mod6,outw,up,zpd,taps,ml,mr,rl,side,cols,T=512):
+    cells,feat=x.shape
+    hidden=up.shape[1]
+    vm=lambda shape: pl.BlockSpec(shape,lambda t:(0,)*len(shape),pipeline_mode=pl.Buffered(1))
+    r_,d_=feat//NDEV,hidden//NDEV
+    return pl.pallas_call(
+        functools.partial(ffn_kernel_body,side=side,cols=cols),
+        grid=(hidden//T,),
+        in_specs=[vm((cells,feat)),vm((cells,feat)),vm((cells,feat)),vm((8,feat)),vm((feat,feat)),
+                  pl.BlockSpec((feat,T),lambda t:(0,t)),HBM,pl.BlockSpec((16,T),lambda t:(0,t)),
+                  vm((cells,128)),vm((cells,128)),SM],
+        out_specs=[vm((cells,feat)),vm((cells,feat)),vm((cells,feat)),vm((feat,feat)),
+                   vm((NZ,r_,hidden)),vm((NZ,d_,feat)),pl.BlockSpec((16,T),lambda t:(0,t)),vm((8,feat))],
+        out_shape=[S_((cells,feat),BF),S_((cells,feat),F32),S_((cells,feat),BF),S_((feat,feat),BF),S_((NZ,r_,hidden),BF),S_((NZ,d_,feat),BF),S_((16,hidden),F32),S_((8,feat),F32)],
+        scratch_shapes=[pltpu.VMEM((cells,feat),BF),pltpu.VMEM((feat,cells),BF),pltpu.VMEM((cells,feat),BF),
+                        pltpu.VMEM((cells,feat),F32),pltpu.VMEM((cells,feat),F32),pltpu.VMEM((cells,feat),F32),pltpu.VMEM((cells,feat),F32),
+                        pltpu.VMEM((cells,T),F32),pltpu.VMEM((cells,T),F32),pltpu.VMEM((cells,T),BF),pltpu.VMEM((cells,T),BF),
+                        pltpu.VMEM((NZ,NC,NR,d_,feat),BF),pltpu.VMEM((NZ,NC,NR,d_,feat),BF)]
+                       +PipeScatter.scratch(r_,T)+RowScatter.scratch(d_,feat)
+                       +sem_types(GatherXY.SEMS)+sem_types(PipeScatter.SEMS)+sem_types(RowScatter.SEMS),
+        compiler_params=pltpu.CompilerParams(dimension_semantics=("arbitrary",),vmem_limit_bytes=63<<20,collective_id=4,has_side_effects=True),
+        name="ffn",
+    )(x,att,cot,mod6,outw,up,zpd,taps,ml,mr,rl)
 def own_rows(padded_cells):
     return jnp.pad(padded_cells,((0,0),(1,1),(1,1),(0,0)))
 
@@ -836,77 +1339,48 @@
     cells=side*cols
     rows=lax.axis_index("rows"); dp=lax.axis_index("dp"); me=dp*NR+rows
     hidden=up_weight.shape[1]
-    cond_row=lax.dynamic_slice_in_dim(conditioning,rows,1,0)
-    cond_row8=jnp.pad(cond_row,((0,7),(0,0)))
+    cond_row=jnp.pad(lax.dynamic_slice_in_dim(conditioning,rows,1,0),((0,7),(0,0)))
     mod_cols=ada_weight.shape[1]
     bshard=ada_bias.shape[0]
     bias_rows=lax.dynamic_update_slice_in_dim(jnp.zeros((mod_cols,),F32),ada_bias.astype(F32),me*bshard,0).reshape(mod_cols//128,128)
-    pad8=(-(mod_cols//128))%8
-    taps=jnp.pad(jnp.concatenate([attn_kernel,ffn_kernel],axis=1),((0,7),(0,128-attn_kernel.shape[1]-ffn_kernel.shape[1])))
     ta,tf=attn_kernel.shape[1],ffn_kernel.shape[1]
-    tok,cot,low_all,mod,qkv_f,taps_f,out_f,up_f,down_f=enter(
-        tokens.reshape(NR,rows_here*cols,features),out_cotangent.reshape(NR,rows_here*cols,features),
-        cond_row8,ada_weight,bias_rows,[qkv_weight,taps,out_weight,up_weight,down_weight])
+    taps=jnp.pad(jnp.concatenate([attn_kernel,ffn_kernel],axis=1),((0,7),(0,128-ta-tf)))
+    blocks=(NR,rows_here*cols,features)
+    tok,low_all,mod,qkv_f,taps_f,*zps=enter(tokens.reshape(blocks),cond_row,ada_weight,bias_rows,qkv_weight,taps,[out_weight,up_weight])
     full2=lambda a:a.reshape(-1,a.shape[-1])
-    triple_full,out_full,up_full,down_full=full2(qkv_f),full2(out_f),full2(up_f),full2(down_f)
+    triple_full=full2(qkv_f)
     taps_f=taps_f.reshape(NDEV,16,128)[:,:9]
     kernel_attn=taps_f[:,:,:ta].transpose(1,0,2).reshape(9,features)
     kernel_ffn=taps_f[:,:,ta:ta+tf].transpose(1,0,2).reshape(9,hidden)
     labels=lax.dynamic_slice_in_dim(item_map,rows,1,0)
     labels_pad=jnp.pad(labels,((0,0),(1,1),(1,1)),constant_values=-1)
-    shift1,scale1,gate1,shift2,scale2,gate2=(mod.reshape(6,features)[i][None,None,None] for i in range(6))
+    qm,km=head_masks(labels.reshape(cells))
+    ml,mr,rl=link_masks(labels[0])
+    mod6=mod.reshape(6,features)
+    shift1,scale1,gate1,shift2,scale2,gate2=(mod6[i][None,None,None] for i in range(6))
     x=tok.reshape(1,side,cols,features).astype(F32)
-    incoming=cot.reshape(1,side,cols,features).astype(F32)
     n1,i1=normalize(x)
     m1=(n1*(1.0+scale1)+shift1).astype(BF)
     m1p=own_rows(m1)
     mix=conv_forward(m1p,labels_pad,labels,kernel_attn).astype(BF).reshape(cells,features)
-    projected=jnp.dot(mix,triple_full,preferred_element_type=F32).astype(BF)
-    qm,km=head_masks(labels.reshape(cells))
-    attended,lse=attn_fwd(projected,qm,km,features)
-    branch=jnp.dot(attended,out_full,preferred_element_type=F32).reshape(x.shape)
-    middle=x+gate1*branch
-    n2,i2=normalize(middle)
-    m2=(n2*(1.0+scale2)+shift2).astype(BF)
-    m2r=m2.reshape(cells,features)
-    hid=jnp.dot(m2r,up_full,preferred_element_type=F32).astype(BF).reshape(1,side,cols,hidden)
-    hidp=own_rows(hid)
-    pre=conv_forward(hidp,labels_pad,labels,kernel_ffn)
-    act,gback=jax.vjp(jax.nn.gelu,pre)
-    glow=act.astype(BF).reshape(cells,hidden)
-    fbranch=jnp.dot(glow,down_full,preferred_element_type=F32).reshape(x.shape)
-    layer_out=(middle+gate2*fbranch).astype(BF)
-    g_gate2=jnp.sum(incoming*fbranch,axis=(1,2))
-    gffn=(gate2*incoming).astype(BF).reshape(cells,features)
-    g_down=contract_rows(glow,gffn)
-    ggelu=contract_cols(gffn,down_full).reshape(1,side,cols,hidden)
-    gpre=gback(ggelu)[0].astype(BF)
-    gprep=own_rows(gpre)
-    g_kffn=kernel_grad(gpre,hidp,labels_pad,labels)
-    gup=conv_mirror(gprep,labels_pad,labels,kernel_ffn).astype(BF).reshape(cells,hidden)
-    g_up=contract_rows(m2r,gup)
-    gm2=contract_cols(gup,up_full).reshape(x.shape)
-    g_scale2=jnp.sum(gm2*n2,axis=(1,2)); g_shift2=jnp.sum(gm2,axis=(1,2))
-    gmid=incoming+normalize_back(gm2*(1.0+scale2),n2,i2)
-    g_gate1=jnp.sum(gmid*branch,axis=(1,2))
-    gattn=(gate1*gmid).astype(BF).reshape(cells,features)
-    g_out=contract_rows(attended,gattn)
-    gatt=contract_cols(gattn,out_full).astype(BF)
-    dq,dk,dv=attn_bwd(projected,gatt,attended,qm,km,lse.T,features)
-    gproj=jnp.concatenate([dq,dk,dv],axis=1)
-    g_qkv=contract_rows(mix,gproj)
+    proj,attended,lse_t,cot,zp_down,out_f,up_f=forward(mix,triple_full,qm,km,out_cotangent.reshape(blocks),down_weight,zps)
+    lay,gmid,gatt,g_out,z_up,z_down,g_kffn,sums=ffn(
+        tok.reshape(cells,features),attended,cot.reshape(cells,features),jnp.pad(mod6,((0,2),(0,0))),
+        full2(out_f),full2(up_f),zp_down,jnp.pad(kernel_ffn,((0,7),(0,0))),ml,mr,rl,side,cols)
+    sp=lambda g:g.reshape(NZ,NC,NR,g.shape[0]//NDEV,g.shape[1])
+    gproj,lay_o,o_o,u_o,d_o=backward(proj,gatt,attended,qm,km,lse_t,lay.reshape(blocks),sp(g_out),[z_up,z_down])
+    g_gate2,g_shift2,g_scale2,g_gate1=(sums[i:i+1] for i in range(4))
+    gmid=gmid.reshape(x.shape)
+    g_qkv=contract_rows(mix,gproj).astype(BF)
     gmix=contract_cols(gproj,triple_full).astype(BF).reshape(x.shape)
     g_kattn=kernel_grad(gmix,m1p,labels_pad,labels)
     gm1=conv_mirror(own_rows(gmix),labels_pad,labels,kernel_attn)
     g_scale1=jnp.sum(gm1*n1,axis=(1,2)); g_shift1=jnp.sum(gm1,axis=(1,2))
     tgrad=gmid+normalize_back(gm1*(1.0+scale1),n1,i1)
     gmod=jnp.concatenate([g_shift1,g_scale1,g_gate1,g_shift2,g_scale2,g_gate2],axis=-1).astype(BF)
-    gtaps=jnp.concatenate([g_kattn.reshape(9,NDEV,ta),g_kffn.reshape(9,NDEV,tf)],axis=2).transpose(1,0,2)
+    gtaps=jnp.concatenate([g_kattn.reshape(9,NDEV,ta),g_kffn[:9].reshape(9,NDEV,tf)],axis=2).transpose(1,0,2)
     gtaps=jnp.pad(gtaps,((0,0),(0,7),(0,128-ta-tf))).reshape(NZ,NC,NR,16,128)
-    sp=lambda g:g.astype(BF).reshape(NZ,NC,NR,g.shape[0]//NDEV,g.shape[1])
-    lay,tg,ctx,adag,gmsum,q_o,t_o,o_o,u_o,d_o=leave(
-        layer_out.reshape(NR,rows_here*cols,features),tgrad.astype(BF).reshape(NR,rows_here*cols,features),
-        gmod.reshape(mod_cols//128,128),low_all,ada_weight,[sp(g_qkv),gtaps,sp(g_out),sp(g_up),sp(g_down)])
+    tg,ctx,adag,gmsum,q_o,t_o=leave(tgrad.astype(BF).reshape(blocks),gmod.reshape(mod_cols//128,128),low_all,ada_weight,[sp(g_qkv),gtaps])
     shape4=(NR,rows_here,cols,features)
     feats=ada_weight.shape[0]
     dsilu=ctx[:,:NR,:feats].transpose(1,0,2).reshape(NR,features)
@@ -914,7 +1388,7 @@
     _,sback=jax.vjp(jax.nn.silu,cv)
     dctx=sback(dsilu)[0]
     gbias=lax.dynamic_slice_in_dim(gmsum.reshape(mod_cols),me*bshard,bshard,0)
-    return (lay.reshape(shape4),tg.reshape(shape4).astype(F32),dctx,adag,gbias,t_o[:9,:ta],q_o,o_o,u_o,t_o[:9,ta:ta+tf],d_o)
+    return (lay_o.reshape(shape4),tg.reshape(shape4).astype(F32),dctx,adag,gbias,t_o[:9,:ta],q_o,o_o,u_o,t_o[:9,ta:ta+tf],d_o)
 
 
 def solution(mesh):

time: 662 us -> 472 us (0.71); the launches traced: 653 us -> 472 us
  other arithmetic: 134 us -> 31.5 us
  matrix products: 121 us -> 19.6 us
  Pallas kernels: 362 us -> 392 us
    convert_element_type x4 -> x2, other arithmetic: 93.5 us -> 2.11 us  [the longest x1 2.04 us: fast(): tgrad.astype(BF).reshape(blocks)]
    dot_general x4 -> x1, matrix products: 70.4 us -> 11.8 us  [contract_cols(): lax.dot_general(left, right, (((1,), (1,)), ((), ())), preferred_element_...]
    pallas_call x4 -> x5, Pallas kernels: 362 us -> 392 us  [the longest x1 147 us: ffn(): pl.pallas_call(functools.partial(ffn_kernel_body, side=side, cols=cols),...]
    dot_general x4 -> x0, matrix products: 26.2 us -> none  [the longest x1 8.66 us: fast(): jnp.dot(glow, down_full, preferred_element_type=F32).reshape(x.shape)]
    dot_general x4 -> x1, matrix products: 24.9 us -> 7.78 us  [contract_rows(): lax.dot_general(left, right, (((0,), (0,)), ((), ())), preferred_element_...]
    unnamed x199 -> x76, local copies, waits for them, and re-layouts: 24 us -> 13.6 us
where the time goes in v2:
time: 472 us
  Pallas kernels  392 us (83%)
  other arithmetic  31.5 us (7%)
  local copies, waits for them, and re-layouts  27.2 us (6%)
  matrix products  19.6 us (4%)
    pallas_call x1, Pallas kernels, ffn(): pl.pallas_call(functools.partial(ffn_kernel_body, side=side, cols=cols),...  147 us
    pallas_call x1, Pallas kernels, forward(): pl.pallas_call(functools.partial(forward_kernel, n, 256), in_specs=[VM, V...  67.6 us
    pallas_call x1, Pallas kernels, leave(): pl.pallas_call(functools.partial(leave_kernel, n_g), in_specs=[HBM, HBM,...  64.1 us
    pallas_call x1, Pallas kernels, backward(): pl.pallas_call(functools.partial(backward_kernel, n, 256), in_specs=[VM,...  57.1 us
    pallas_call x1, Pallas kernels, enter(): pl.pallas_call(functools.partial(enter_kernel, n), in_specs=[HBM, HBM, VM...  56.5 us
    unnamed x76, local copies, waits for them, and re-layouts  13.6 us
    dot_general x1, matrix products, contract_cols(): lax.dot_general(left, right, (((1,), (1,)), ((), ())), preferred_element_...  11.8 us

profile of v2, /device:TPU:0, one launch (start us, length us, event | category | flops | bytes accessed | tf_op | source)
XLA Modules:
  0.0 471.6 jit_solution(6454792934814495702)
XLA Ops:
  1.4 0.8 fusion.66.refs_5_
  3.3 0.8 convert_dynamic-update-slice_fusion
  4.3 0.9 select_convert_fusion.refs_3_.refs_4_
  5.2 0.9 fusion.38.refs_2_.refs_3_
  6.1 1.0 broadcast_in_dim.236.refs_8_
  7.1 1.0 broadcast_in_dim.237.refs_9_
  8.1 1.4 copy-done.4
  9.5 0.9 copy-done.5
  10.5 0.9 copy-done.7
  11.4 0.9 copy-done.9
  12.3 0.8 copy-done.11
  13.0 56.5 %enter.1 = (bf16[4,256,768]{2,1,0:T(8,128)(2,1)S(1)}, bf16[32,768]{1,0:T(8,128)(2,1)S(1)}, f32[36,128]{1,0:T(8,128)S(1)}, bf16[4,2,4,24,2304]{4,3,2,1,0:T(8,128)...) custom-call(bf16[4,256,768]{2,1,0:T(8,128)(2,1)S(1)} %bitcast.80, ...), custom_call_target="tpu_custom_call" | custom-call | tf_op jit(solution)/shard_map/enter/pallas_call | solution.py:843
  69.5 0.8 copy-done.6
  75.1 2.3 add_convert_fusion.2
  77.4 1.2 copy-done.13
  78.6 7.6 %fusion.9 = bf16[1,32,32,768]{3,2,1,0:T(8,128)(2,1)} fusion(bf16[1,32,32,768]{3,2,1,0:T(8,128)(2,1)S(1)} %get-tuple-element.90, f32[768]{0:T(1024)S(1)} %reshape.496, f32[768]{0:T(1024)S(1)} %reshape.495, f32[768]{0:T(1024)S(1)} %reshape.494, f32[768]{0:T(1024)S(1)} %reshape.493, f32[768]{0:T(1024)S(1)} %reshape.492, f32[768]{0:T(1024)S(1)} %reshape.491, ...), kind=kLoop, calls=%fused_computation.27 | loop fusion | flops 27525120 | bytes 3181568 | tf_op jit(solution)/shard_map/convert_element_type | solution.py:1365
  86.2 67.6 %attn_fwd.1 = (bf16[1024,2304]{1,0:T(8,128)(2,1)}, bf16[1024,768]{1,0:T(8,128)(2,1)}, f32[128,1024]{1,0:T(8,128)}, bf16[4,256,768]{2,1,0:T(8,128)(2,1)}, bf16[4,...) custom-call(bf16[1024,768]{1,0:T(8,128)(2,1)} %bitcast.86, ...), custom_call_target="tpu_custom_call" | custom-call | tf_op jit(solution)/shard_map/attn_fwd/pallas_call | solution.py:918
  153.7 146.8 %ffn.1 = (bf16[1024,768]{1,0:T(8,128)(2,1)}, f32[1024,768]{1,0:T(8,128)}, bf16[1024,768]{1,0:T(8,128)(2,1)}, bf16[768,768]{1,0:T(8,128)(2,1)}, bf16[4,24,3072]{2...) custom-call(bf16[1024,768]{1,0:T(8,128)(2,1)} %bitcast.79, ...), custom_call_target="tpu_custom_call" | custom-call | tf_op jit(solution)/shard_map/ffn/pallas_call | solution.py:1314
  300.5 57.1 %attn_bwd.1 = (bf16[1024,2304]{1,0:T(8,128)(2,1)}, bf16[4,256,768]{2,1,0:T(8,128)(2,1)}, f32[24,768]{1,0:T(8,128)}, f32[24,3072]{1,0:T(8,128)}, f32[96,768]{1,0:T(8,128)}) custom-call(bf16[1024,2304]{1,0:T(8,128)(2,1)} %get-tuple-element.50.refs_0_, bf16[1024,768]{1,0:T(8,128)(2,1)} %get-tuple-element.56.refs_1_, ...), custom_call_target="tpu_custom_call" | custom-call | tf_op jit(solution)/shard_map/attn_bwd/pallas_call | solution.py:1007
  357.7 11.8 %fusion.37 = (f32[768]{0:T(1024)S(1)}, f32[768]{0:T(1024)S(1)}, f32[768]{0:T(1024)S(1)}, f32[768]{0:T(1024)S(1)}, f32[768]{0:T(1024)S(1)}, /*index=5*/f32[768]{0...) fusion(pred[32,32]{1,0:T(8,128)(4,1)S(1)} %get-tuple-element.104, ...), kind=kOutput, calls=%fused_computation.55 | convolution fusion | flops 3650611200 | bytes 11436032 | tf_op jit(solution)/shard_map/dot_general | solution.py:112
  369.5 1.0 multiply_reduce_fusion
  371.5 1.7 reshape.483
  373.2 1.0 copy.33
  375.0 7.8 %convolution_convert_fusion = bf16[768,2304]{1,0:T(8,128)(2,1)} fusion(bf16[1024,768]{1,0:T(8,128)(2,1)S(1)} %bitcast.87, bf16[1024,2304]{1,0:T(8,128)(2,1)} %get-tuple-element.64), kind=kOutput, calls=%fused_computation.9 | convolution fusion | flops 3625648128 | bytes 9830400 | tf_op jit(solution)/shard_map/dot_general | solution.py:106
  382.8 8.5 %multiply_reduce_fusion.1 = (bf16[768]{0:T(1024)(128)(2,1)S(1)}, f32[32,32]{1,0:T(8,128)S(1)}, f32[32,32]{1,0:T(8,128)S(1)}, bf16[768]{0:T(1024)(128)(2,1)S(1)}, f32[1,32,32,768]{3,2,1,0:T(8,128)S(1)}) fusion(f32[1,32,32,768]{3,2,1,0:T(8,128)S(1)} %copy-done.12, f32[32,32]{1,0:T(8,128)S(1)} %rsqrt.16, f32[32,32]{1,0:T(8,128)S(1)} %div.31, ...), kind=kLoop, calls=%fused_computation.58 | loop fusion | flops 33812992 | bytes 7922688 | tf_op jit(solution)/shard_map/reduce_sum | solution.py:1378
  391.3 2.0 add_convert_fusion.1
  394.1 64.1 %leave.1 = (bf16[4,256,768]{2,1,0:T(8,128)(2,1)}, f32[32,8,128]{2,1,0:T(8,128)}, f32[24,4608]{1,0:T(8,128)}, f32[36,128]{1,0:T(8,128)}, f32[24,2304]{1,0:T(8,128)}, /*index=5*/f32[16,128]{1,0:T(8,128)}) custom-call(bf16[4,256,768]{2,1,0:T(8,128)(2,1)} %bitcast.84, bf16[36,128]{1,0:T(8,128)(2,1)} %bitcast.104, bf16[32,768]{1,0:T(8,128)(2,1)} %copy-done.10, ...), custom_call_target="tpu_custom_call" | custom-call | tf_op jit(solution)/shard_map/leave/pallas_call | solution.py:1068
  458.3 1.5 dynamic_slice.11
  459.7 1.4 slice.258
  461.1 0.9 slice_bitcast_fusion
  462.8 3.5 convert.36
  466.3 1.1 copy.64
  (128 shorter events, 14.0 us)
Async XLA Ops:
  0.6 1.5 copy-start
  8.1 1.4 copy-start.4
  9.5 0.9 copy-start.5
  10.5 0.9 copy-start.7
  11.4 0.9 copy-start.9
  12.3 0.8 copy-start.11
  69.5 0.8 copy-start.6
  70.3 0.7 copy-start.8
  71.0 0.6 copy-start.10
  71.6 5.8 %copy-start.2 = (bf16[4,256,768]{2,1,0:T(8,128)(2,1)}, bf16[4,256,768]{2,1,0:T(8,128)(2,1)S(1)}, u32[]{:S(2)}) copy-start(bf16[4,256,768]{2,1,0:T(8,128)(2,1)S(1)} %get-tuple-element.45) | copy-start | bytes 4718596
  77.4 1.2 copy-start.13
  300.5 57.1 %copy-start.14 = (bf16[1,32,32,768]{3,2,1,0:T(8,128)(2,1)S(1)}, bf16[1,32,32,768]{3,2,1,0:T(8,128)(2,1)}, u32[]{:S(2)}) copy-start(bf16[1,32,32,768]{3,2,1,0:T(8,128)(2,1)} %copy-done.13) | copy-start | bytes 4718596
  357.7 11.9 %copy-start.3 = (bf16[4,256,768]{2,1,0:T(8,128)(2,1)S(1)}, bf16[4,256,768]{2,1,0:T(8,128)(2,1)}, u32[]{:S(2)}) copy-start(bf16[4,256,768]{2,1,0:T(8,128)(2,1)} %copy-done.2) | copy-start | bytes 4718596
  369.5 1.0 copy-start.24
  369.5 5.5 %copy-start.15 = (bf16[1,32,32,768]{3,2,1,0:T(8,128)(2,1)S(1)}, bf16[1,32,32,768]{3,2,1,0:T(8,128)(2,1)}, u32[]{:S(2)}) copy-start(bf16[1,32,32,768]{3,2,1,0:T(8,128)(2,1)} %fusion.9) | copy-start | bytes 4718596
  375.0 7.8 %copy-start.12 = (f32[1,32,32,768]{3,2,1,0:T(8,128)S(1)}, f32[1,32,32,768]{3,2,1,0:T(8,128)}, u32[]{:S(2)}) copy-start(f32[1,32,32,768]{3,2,1,0:T(8,128)} %get-tuple-element.91) | copy-start | bytes 9437188
  382.8 8.5 %copy-start.16 = (f32[1024,768]{1,0:T(8,128)S(1)}, f32[1024,768]{1,0:T(8,128)}, u32[]{:S(2)}) copy-start(f32[1024,768]{1,0:T(8,128)} %get-tuple-element.63) | copy-start | bytes 9437188
  393.4 68.8 %copy-start.25 = (bf16[4,768]{1,0:T(4,128)(2,1)S(1)}, bf16[4,768]{1,0:T(4,128)(2,1)}, u32[]{:S(2)}) copy-start(bf16[4,768]{1,0:T(4,128)(2,1)} %param.13) | copy-start | bytes 18436
  458.3 8.0 %copy-start.17 = (bf16[4,256,768]{2,1,0:T(8,128)(2,1)S(1)}, bf16[4,256,768]{2,1,0:T(8,128)(2,1)}, u32[]{:S(2)}) copy-start(bf16[4,256,768]{2,1,0:T(8,128)(2,1)} %get-tuple-element.62) | copy-start | bytes 4718596
  462.8 4.7 copy-start.18
  462.8 8.8 %copy-start.1 = (s32[4,32,32]{2,1,0:T(8,128)S(1)}, s32[4,32,32]{2,1,0:T(8,128)}, u32[]{:S(2)}) copy-start(s32[4,32,32]{2,1,0:T(8,128)} %param.14) | copy-start | bytes 49156
  466.3 1.9 copy-start.23
  466.3 2.5 copy-start.21
  466.3 3.2 copy-start.22
  466.3 3.9 copy-start.20
  466.3 4.6 copy-start.19
